TPU v7x, 128 devices: a whole 4x4x4 slice. The times are simulated.
128 devices in a mesh: head: 8 (over z, y_lo), pts: 16 (over y_hi, x, core).
Axes of the slice: x: 4, y: 4 (y_hi: 2, y_lo: 2; y = y_hi * 2 + y_lo), z: 4, core: 2. Of those that a mesh axis runs over, the one named last changes fastest.
Arguments:
- layer_inputs_trainorder: bfloat16 [786432, 256], P(('head', 'pts')), may hold values from -6 to 6
- inference_placement: int32 [786432], P(('head', 'pts')), may hold values from 0 to 786431, as said below
- initial_layernorm_gain: float32 [256], replicated, may hold values from 0.1 to 1.9
- initial_layernorm_offset: float32 [256], replicated, may hold values from -2 to 2
- attribute_projection: bfloat16 [256, 256], replicated, may hold values from -0.375 to 0.375
- assignment_feeder_projection: bfloat16 [256, 256], replicated, may hold values from -0.375 to 0.375
- partition_projection: bfloat16 [16, 32], replicated, may hold values from -1.5 to 1.5
- partition_offset: float32 [32], replicated, may hold values from -4 to 4
- softmax_sharpness: float32 [16], P('head'), may hold values from 0.03 to 1
- partition_question_map: float32 [16, 16], replicated, may hold values from -1.5 to 1.5
- partition_lookup_map: float32 [16, 16], replicated, may hold values from -1.5 to 1.5
- partition_content_map: float32 [16, 16], replicated, may hold values from -1.5 to 1.5
- emitted_projection: bfloat16 [256, 256], replicated, may hold values from -0.375 to 0.375
- emitted_offset: float32 [256], replicated, may hold values from -2 to 2
- latter_layernorm_gain: float32 [256], replicated, may hold values from 0.1 to 1.9
- latter_layernorm_offset: float32 [256], replicated, may hold values from -2 to 2
- perceptron_entry_map: bfloat16 [256, 1024], replicated, may hold values from -0.375 to 0.375
- perceptron_entry_offset: float32 [1024], replicated, may hold values from -2 to 2
- perceptron_exit_map: bfloat16 [1024, 256], replicated, may hold values from -0.1875 to 0.1875
- perceptron_exit_offset: float32 [256], replicated, may hold values from -2 to 2
Outputs:
- served: bfloat16 [16, 49152, 256], P('pts', 'head')
Inputs may be any that keep to these rules, and one draw needn't show every extreme that they name: inference_placement is a permutation of all points; of the 6144 points of each aligned block of the training order, exactly 48 go to each aligned block of 6144 serving positions.
All inputs are finite; a program needn't handle non-finite values.
Results may differ from a plain program's by a relative error of at most 0.0035.
The roundings to bfloat16 on the way count: a program that leaves them out, or rounds other values in their place, can miss the bound.
Values may be sent and summed in bfloat16 or wider, within the bound.
A program may use at most 128 MiB of HBM per device.

v0:
```python
import math

import jax
import jax.numpy as jnp
from jax import lax
from jax.sharding import Mesh
from jax.sharding import PartitionSpec as P

DH = 16
HEAD_PTS = ("head_0", "head_1", "pts_0", "pts_1", "pts_2")
HEAD = ("head_0", "head_1")
PTS = ("pts_0", "pts_1", "pts_2")


def from_everyone(array, axis):
    copies = jnp.broadcast_to(array, (lax.axis_size(axis), *array.shape))
    return lax.all_to_all(copies, axis, split_axis=0, concat_axis=0, tiled=True)


def in_order(tiles, dim):
    tiles = jnp.moveaxis(tiles, 0, dim)
    dims = tiles.shape
    return tiles.reshape(*dims[:dim], dims[dim] * dims[dim + 1], *dims[dim + 2 :])


def gather_directly(array, axis, dim):
    tiles = from_everyone(array, axis)
    return in_order(tiles, dim)


def one_axis_at_a_time(array, axes):
    for axis in axes:
        array = lax.psum(array, axis)
    return array


def layer_norm(row_block, gain_vec, bias_vec):
    row_mean = jnp.mean(row_block, axis=-1, keepdims=True)
    centred = row_block - row_mean
    spread = jnp.mean(centred * centred, axis=-1, keepdims=True)
    return centred * lax.rsqrt(spread + 1e-05) * gain_vec + bias_vec


def move_rows(rows, labels, ordering):
    arrived = lax.all_to_all(rows[ordering], HEAD_PTS, split_axis=0, concat_axis=0, tiled=True)
    arrived_labels = lax.all_to_all(labels, HEAD_PTS, split_axis=0, concat_axis=0, tiled=True)
    placed = jnp.argsort(arrived_labels[:, 0])
    return (arrived[placed], arrived_labels[placed, 1])


def slice_attention(
    totals, numerator, partition_question_map, partition_lookup_map, partition_content_map
):
    slice_token = numerator / (totals + 1e-05)[:, :, None]
    highest_mode = lax.Precision.HIGHEST
    query_rows = jnp.einsum(
        "izn,nu->izu", slice_token, partition_question_map, precision=highest_mode
    )
    key_vectors = jnp.einsum(
        "izn,nu->izu", slice_token, partition_lookup_map, precision=highest_mode
    )
    value_rows = jnp.einsum(
        "izn,nu->izu", slice_token, partition_content_map, precision=highest_mode
    )
    score_scale = 1.0 / math.sqrt(DH)
    scores = (
        jnp.einsum("hme,hne->hmn", query_rows, key_vectors, precision=highest_mode) * score_scale
    )
    attention = jax.nn.softmax(scores, axis=-1)
    return jnp.einsum("hmn,hne->hme", attention, value_rows, precision=highest_mode).astype(
        jnp.bfloat16
    )


def finish_rows(
    residual_rows,
    blended_rows,
    emitted_projection,
    emitted_offset,
    latter_layernorm_gain,
    latter_layernorm_offset,
    perceptron_entry_map,
    perceptron_entry_offset,
    perceptron_exit_map,
    perceptron_exit_offset,
):
    hidden = (
        residual_rows.astype(jnp.float32)
        + jnp.dot(blended_rows, emitted_projection, preferred_element_type=jnp.float32)
        + emitted_offset
    )
    normed_two = layer_norm(hidden, latter_layernorm_gain, latter_layernorm_offset).astype(
        jnp.bfloat16
    )
    inner_act = jax.nn.gelu(
        jnp.dot(normed_two, perceptron_entry_map, preferred_element_type=jnp.float32)
        + perceptron_entry_offset,
        approximate=False,
    ).astype(jnp.bfloat16)
    return (
        hidden
        + jnp.dot(inner_act, perceptron_exit_map, preferred_element_type=jnp.float32)
        + perceptron_exit_offset
    ).astype(jnp.bfloat16)


def body(
    layer_inputs_trainorder,
    inference_placement,
    initial_layernorm_gain,
    initial_layernorm_offset,
    attribute_projection,
    assignment_feeder_projection,
    partition_projection,
    partition_offset,
    softmax_sharpness,
    partition_question_map,
    partition_lookup_map,
    partition_content_map,
    emitted_projection,
    emitted_offset,
    latter_layernorm_gain,
    latter_layernorm_offset,
    perceptron_entry_map,
    perceptron_entry_offset,
    perceptron_exit_map,
    perceptron_exit_offset,
):
    groups = lax.axis_size(HEAD)
    shards = lax.axis_size(PTS)
    local_rows = layer_inputs_trainorder.shape[0]
    model_width = layer_inputs_trainorder.shape[1]
    dest_block = inference_placement // local_rows
    target = dest_block % groups * shards + dest_block // groups
    ordering = jnp.argsort(target, stable=True)
    anchor = lax.axis_index(HEAD_PTS) * local_rows + jnp.arange(local_rows, dtype=jnp.int32)
    labels = jnp.stack([inference_placement[ordering], anchor[ordering]], axis=1)
    sharpness_sequence = gather_directly(softmax_sharpness, HEAD, 0)
    every_attender = sharpness_sequence.shape[0]
    standardized_entries = layer_norm(
        layer_inputs_trainorder.astype(jnp.float32),
        initial_layernorm_gain,
        initial_layernorm_offset,
    ).astype(jnp.bfloat16)
    slice_feature_rows = (
        jnp.dot(standardized_entries, attribute_projection, preferred_element_type=jnp.float32)
        .astype(jnp.bfloat16)
        .reshape(local_rows, every_attender, DH)
    )
    middle = (
        jnp.dot(
            standardized_entries, assignment_feeder_projection, preferred_element_type=jnp.float32
        )
        .astype(jnp.bfloat16)
        .reshape(local_rows, every_attender, DH)
    )
    partition_scores_raw = jnp.einsum(
        "rhd,dm->rhm", middle, partition_projection, preferred_element_type=jnp.float32
    )
    partition_scores_raw = (partition_scores_raw + partition_offset) / sharpness_sequence[:, None]
    coefficient_array = jax.nn.softmax(partition_scores_raw, axis=-1)
    coefficients_halfprecision = coefficient_array.astype(jnp.bfloat16)
    totals = jnp.sum(coefficient_array, axis=0)
    numerator = jnp.einsum(
        "qct,qcv->ctv",
        coefficients_halfprecision,
        slice_feature_rows,
        preferred_element_type=jnp.float32,
    )
    totals, numerator = (
        one_axis_at_a_time(totals, HEAD_PTS),
        one_axis_at_a_time(numerator, HEAD_PTS),
    )
    slice_output = slice_attention(
        totals, numerator, partition_question_map, partition_lookup_map, partition_content_map
    )
    blended_rows = (
        jnp.einsum(
            "fny,nyp->fnp",
            coefficients_halfprecision,
            slice_output,
            preferred_element_type=jnp.float32,
        )
        .astype(jnp.bfloat16)
        .reshape(local_rows, model_width)
    )
    result = finish_rows(
        layer_inputs_trainorder,
        blended_rows,
        emitted_projection,
        emitted_offset,
        latter_layernorm_gain,
        latter_layernorm_offset,
        perceptron_entry_map,
        perceptron_entry_offset,
        perceptron_exit_map,
        perceptron_exit_offset,
    )
    served, unused = move_rows(result, labels, ordering)
    return served[None]


def solution(mesh):
    torus = Mesh(
        mesh.devices.reshape(4, 2, 2, 4, 2), ("head_0", "head_1", "pts_0", "pts_1", "pts_2")
    )
    in_specs = (
        P(HEAD_PTS, None),
        P(HEAD_PTS),
        P(),
        P(),
        P(),
        P(),
        P(),
        P(),
        P(HEAD),
        P(),
        P(),
        P(),
        P(),
        P(),
        P(),
        P(),
        P(),
        P(),
        P(),
        P(),
    )
    out_specs = P(PTS, HEAD, None)
    return jax.shard_map(body, mesh=torus, in_specs=in_specs, out_specs=out_specs, check_vma=False)
```

profile of v0, /device:TPU:1, one launch (start us, length us, event | category | flops | bytes accessed | tf_op | source)
XLA Modules:
  0.0 388.4 jit_solution(6724094378203701550)
XLA Ops:
  0.0 0.0 copy-start
  0.0 0.0 copy-start.12
  0.0 1.3 broadcast_in_dim.8
  1.3 6.9 %all-to-all-start = ((f32[8,1,2]{2,1,0:T(1,128)}), f32[8,1,2]{2,1,0:T(1,128)S(1)}, u32[]{:S(2)}, u32[]{:S(2)}) async-start(f32[8,1,2]{2,1,0:T(1,128)} %broadcast_in_dim.8), calls=%async_computation | async-start | bytes 8192 | tf_op jit(solution)/shard_map/all_to_all | solution.py:17
  8.2 4.6 %copy.45 = bf16[6144,256]{0,1:T(8,128)(2,1)} copy(bf16[6144,256]{1,0:T(8,128)(2,1)} %param.20) | data formatting | bytes 6291456 | tf_op args[0]
  12.8 2.6 convert_reduce_fusion
  15.4 2.7 fusion.27
  18.2 0.0 copy-done.20
  18.2 0.0 copy-start.2
  18.2 5.3 %convolution_convert_fusion.2 = bf16[6144,256]{0,1:T(8,128)(2,1)} fusion(bf16[256,256]{1,0:T(8,128)(2,1)S(1)} %copy-done.12, bf16[6144,256]{0,1:T(8,128)(2,1)} %copy.45, f32[256]{0:T(256)S(1)} %copy-done.19, f32[256]{0:T(256)S(1)} %copy-done.20, f32[6144]{0:T(1024)S(1)} %add_rsqrt_fusion.1, f32[6144]{0:T(1024)S(1)} %broadcast_multiply_fusion.1), kind=kOutput, calls=%fused_computation.36 | convolution fusion | flops 816316416 | bytes 6473728 | tf_op jit(solution)/shard_map/dot_general | solution.py:151
  23.5 3.4 convolution_convert_fusion.1
  26.9 0.0 copy-done.2
  27.0 6.7 %sort.34 = (s32[6144]{0:T(1024)}, s32[6144]{0:T(1024)S(1)}) sort(s32[6144]{0:T(1024)S(1)} %fusion.46, s32[6144]{0:T(1024)S(1)} %iota.11), dimensions={0}, to_apply=%region_19.20 | sort | flops 79872 | bytes 98304 | tf_op jit(solution)/shard_map/jit(argsort)/sort | solution.py:135
  33.7 34.3 %gather_fusion.1 = s32[6144]{0:T(1024)S(1)} fusion(s32[6144]{0:T(1024)S(1)} %copy-done.2, s32[6144]{0:T(1024)S(1)} %get-tuple-element.27), kind=kCustom, calls=%fused_computation.1 | custom fusion | bytes 73728 | tf_op jit(solution)/shard_map/gather | solution.py:137
  68.0 0.0 copy-start.17
  68.1 0.0 copy-start.24
  68.1 34.3 %gather_fusion.2 = s32[6144]{0:T(1024)S(1)} fusion(s32[6144]{0:T(1024)S(1)} %get-tuple-element.28, s32[6144]{0:T(1024)S(1)} %get-tuple-element.27), kind=kCustom, calls=%fused_computation.2 | custom fusion | bytes 73728 | tf_op jit(solution)/shard_map/gather | solution.py:137
  102.4 0.1 stack.10
  102.4 0.1 stack.9
  102.6 0.8 copy.52
  103.3 0.0 all-to-all-done
  103.3 11.0 %all-to-all-start.2 = ((s32[128,48,2]{1,2,0:T(2,128)}), s32[128,48,2]{1,2,0:T(2,128)}, u32[]{:S(2)}, u32[]{:S(2)}) async-start(s32[128,48,2]{1,2,0:T(2,128)} %copy.52), calls=%async_computation.2 | async-start | bytes 262144 | tf_op jit(solution)/shard_map/all_to_all | solution.py:46
  114.3 0.5 broadcast.103
  114.8 0.6 reduce.3
  115.5 0.1 div.64
  115.6 0.0 copy-done.17
  115.6 10.9 %fusion.93 = (f32[6144,16]{0,1:T(8,128)S(1)}, f32[6144,16,32]{0,2,1:T(8,128)}) fusion(bf16[6144,16,16]{0,2,1:T(8,128)(2,1)} %bitcast.48, f32[16]{0:T(128)S(1)} %div.64, f32[32]{0:T(128)S(1)} %copy-done.24, bf16[16,32]{1,0:T(8,128)(2,1)S(1)} %copy-done.17), kind=kOutput, calls=%fused_computation.125 | convolution fusion | flops 113246240 | bytes 16123072 | tf_op jit(solution)/shard_map/sub | solution.py:161
  126.5 9.1 %fusion.31 = (f32[16,32]{1,0:T(8,128)S(1)}, bf16[6144,16,32]{0,2,1:T(8,128)(2,1)}) fusion(f32[6144,16,32]{0,2,1:T(8,128)} %get-tuple-element.22, f32[6144,16]{0,1:T(8,128)S(1)} %get-tuple-element.21), kind=kLoop, calls=%fused_computation.47 | loop fusion | flops 9436672 | bytes 19269632 | tf_op jit(solution)/shard_map/reduce_sum | solution.py:163
  135.5 4.6 %fusion.98 = f32[16,32,16]{1,2,0:T(8,128)S(1)} fusion(bf16[6144,16,32]{0,2,1:T(8,128)(2,1)} %get-tuple-element.20, bf16[6144,16,16]{0,2,1:T(8,128)(2,1)S(1)} %bitcast.46), kind=kOutput, calls=%fused_computation.128 | convolution fusion | flops 100663296 | bytes 9469952 | tf_op jit(solution)/shard_map/qct,qcv->ctv/dot_general | solution.py:164
  140.1 15.4 %all-reduce.1 = (f32[16,32,16]{1,2,0:T(8,128)S(1)}, f32[16,32]{1,0:T(8,128)S(1)}) all-reduce(f32[16,32,16]{1,2,0:T(8,128)S(1)} %fusion.98, f32[16,32]{1,0:T(8,128)S(1)} %get-tuple-element.19), channel_id=1, replica_groups=mesh['head_0'=4,'head_1'=2,'pts_0'=2,'pts_1'=4,'pts_2'=2] {'head_0'}, use_global_device_ids=true, to_apply=%region_4.5 | all-reduce | flops 8704 | bytes 69632 | tf_op jit(solution)/shard_map/psum | solution.py:33
  155.5 7.7 %all-reduce.4 = (f32[16,32,16]{1,2,0:T(8,128)S(1)}, f32[16,32]{1,0:T(8,128)S(1)}) all-reduce(f32[16,32,16]{1,2,0:T(8,128)S(1)} %get-tuple-element.11, f32[16,32]{1,0:T(8,128)S(1)} %get-tuple-element.12), channel_id=1, replica_groups=mesh['head_0'=4,'head_1'=2,'pts_0'=2,'pts_1'=4,'pts_2'=2] {'head_1'}, use_global_device_ids=true, to_apply=%region_5.6 | all-reduce | flops 8704 | bytes 69632 | tf_op jit(solution)/shard_map/psum | solution.py:33
  163.2 10.4 %all-reduce.3 = (f32[16,32,16]{1,2,0:T(8,128)S(1)}, f32[16,32]{1,0:T(8,128)S(1)}) all-reduce(f32[16,32,16]{1,2,0:T(8,128)S(1)} %get-tuple-element.17, f32[16,32]{1,0:T(8,128)S(1)} %get-tuple-element.18), channel_id=1, replica_groups=mesh['head_0'=4,'head_1'=2,'pts_0'=2,'pts_1'=4,'pts_2'=2] {'pts_0'}, use_global_device_ids=true, to_apply=%region_6.7 | all-reduce | flops 8704 | bytes 69632 | tf_op jit(solution)/shard_map/psum | solution.py:33
  173.7 15.1 %all-reduce = (f32[16,32,16]{1,2,0:T(8,128)S(1)}, f32[16,32]{1,0:T(8,128)S(1)}) all-reduce(f32[16,32,16]{1,2,0:T(8,128)S(1)} %get-tuple-element.15, f32[16,32]{1,0:T(8,128)S(1)} %get-tuple-element.16), channel_id=1, replica_groups=mesh['head_0'=4,'head_1'=2,'pts_0'=2,'pts_1'=4,'pts_2'=2] {'pts_1'}, use_global_device_ids=true, to_apply=%region_7.8 | all-reduce | flops 8704 | bytes 69632 | tf_op jit(solution)/shard_map/psum | solution.py:33
  188.8 15.1 %all-reduce.2 = (f32[16,32,16]{1,2,0:T(8,128)S(1)}, f32[16,32]{1,0:T(8,128)S(1)}) all-reduce(f32[16,32,16]{1,2,0:T(8,128)S(1)} %get-tuple-element.9, f32[16,32]{1,0:T(8,128)S(1)} %get-tuple-element.10), channel_id=1, replica_groups=mesh['head_0'=4,'head_1'=2,'pts_0'=2,'pts_1'=4,'pts_2'=2] {'pts_2'}, use_global_device_ids=true, to_apply=%region_8.9 | all-reduce | flops 8704 | bytes 69632 | tf_op jit(solution)/shard_map/psum | solution.py:33
  203.8 0.0 copy-start.4
  203.9 0.3 fusion.56
  204.2 0.3 fusion.58
  204.5 0.3 fusion.54
  204.8 0.6 fusion.94
  205.5 0.1 fusion.42
  205.5 0.4 convolution_convert_fusion.3
  205.9 3.8 convolution_convert_fusion
  209.7 0.0 copy-start.18
  209.7 0.0 copy-start.21
  209.7 0.0 copy-start.22
  209.8 1.4 fusion.95
  211.2 0.7 multiply_reduce_fusion
  211.9 1.9 copy-done.5
  213.8 0.0 copy-done
  213.8 0.0 copy-start.11
  213.8 0.0 copy-start.23
  213.8 58.5 %fusion.119 = bf16[6144,1024]{1,0:T(8,128)(2,1)} fusion(f32[1024]{0:T(1024)S(1)} %copy-done.18, bf16[256,1024]{1,0:T(8,128)(2,1)S(1)} %copy-done, f32[6144,256]{0,1:T(8,128)S(1)} %get-tuple-element.26, f32[256]{0:T(256)S(1)} %copy-done.21, f32[256]{0:T(256)S(1)} %copy-done.22, f32[6144]{0:T(1024)S(1)} %add_rsqrt_fusion, ...), kind=kOutput, calls=%fused_computation.8.clone.clone.clone.clone.clone.clone.clone.clone.1 | convolution fusion | flops 3644325888 | bytes 19453952 | tf_op jit(solution)/shard_map/dot_general | solution.py:96
  272.4 0.0 copy-done.11
  272.4 15.5 %fusion.22 = bf16[6144,256]{0,1:T(8,128)(2,1)} fusion(f32[6144,256]{0,1:T(8,128)} %copy-done.5, bf16[1024,256]{1,0:T(8,128)(2,1)S(1)} %copy-done.11, f32[256]{0:T(256)S(1)} %copy-done.23, bf16[6144,1024]{1,0:T(8,128)(2,1)} %fusion.119), kind=kOutput, calls=%fused_computation.37 | convolution fusion | flops 3225944064 | bytes 22545408 | tf_op jit(solution)/shard_map/dot_general | solution.py:102
  287.9 3.2 copy.51
  291.1 25.1 %gather_fusion = bf16[6144,256]{1,0:T(8,128)(2,1)} fusion(bf16[6144,256]{1,0:T(8,128)(2,1)S(1)} %copy.51, s32[6144]{0:T(1024)S(1)} %copy-done.8), kind=kCustom, calls=%fused_computation | custom fusion | bytes 6316032 | tf_op jit(solution)/shard_map/gather | solution.py:45
  316.2 0.0 all-to-all-done.2
  316.2 4.7 %all-to-all-start.1 = ((bf16[128,48,256]{2,1,0:T(8,128)(2,1)}), bf16[128,48,256]{2,1,0:T(8,128)(2,1)}, u32[]{:S(2)}, u32[]{:S(2)}) async-start(bf16[128,48,256]{2,1,0:T(8,128)(2,1)} %bitcast.45), calls=%async_computation.1 | async-start | bytes 6291456 | tf_op jit(solution)/shard_map/all_to_all | solution.py:45
  320.9 0.9 copy.53
  321.8 0.1 all_to_all.23
  322.0 6.7 %sort.35 = (s32[6144]{0:T(1024)}, s32[6144]{0:T(1024)S(1)}) sort(s32[6144]{0:T(1024)S(1)} %bitcast.47, s32[6144]{0:T(1024)S(1)} %iota.13), dimensions={0}, to_apply=%region_20.21 | sort | flops 79872 | bytes 98304 | tf_op jit(solution)/shard_map/jit(argsort)/sort | solution.py:47
  328.7 33.4 %all-to-all-done.1 = bf16[128,48,256]{2,1,0:T(8,128)(2,1)} async-done(((bf16[128,48,256]{2,1,0:T(8,128)(2,1)}), bf16[128,48,256]{2,1,0:T(8,128)(2,1)}, u32[]{:S(2)}, u32[]{:S(2)}) %all-to-all-start.1) | async-done | bytes 3145760 | tf_op jit(solution)/shard_map/all_to_all | solution.py:45
  362.1 25.9 %gather_fusion.3 = bf16[6144,256]{1,0:T(8,128)(2,1)} fusion(bf16[6144,256]{1,0:T(8,128)(2,1)} %bitcast.9, s32[6144]{0:T(1024)S(1)} %fusion.48), kind=kCustom, calls=%fused_computation.3 | custom fusion | bytes 6316032 | tf_op jit(solution)/shard_map/gather | solution.py:48
  388.0 0.0 copy-done.1
  (44 shorter events, 0.2 us)
Async XLA Ops:
  0.0 213.8 %copy-start = (bf16[256,1024]{1,0:T(8,128)(2,1)S(1)}, bf16[256,1024]{1,0:T(8,128)(2,1)}, u32[]{:S(2)}) copy-start(bf16[256,1024]{1,0:T(8,128)(2,1)} %param.36) | copy-start | bytes 1572868
  0.0 18.2 %copy-start.20 = (f32[256]{0:T(256)S(1)}, f32[256]{0:T(256)}, u32[]{:S(2)}) copy-start(f32[256]{0:T(256)} %param.22) | copy-start | bytes 3076
  0.0 18.2 %copy-start.19 = (f32[256]{0:T(256)S(1)}, f32[256]{0:T(256)}, u32[]{:S(2)}) copy-start(f32[256]{0:T(256)} %param.23) | copy-start | bytes 3076
  0.0 18.2 %copy-start.12 = (bf16[256,256]{1,0:T(8,128)(2,1)S(1)}, bf16[256,256]{1,0:T(8,128)(2,1)}, u32[]{:S(2)}) copy-start(bf16[256,256]{1,0:T(8,128)(2,1)} %param.25) | copy-start | bytes 393220
  1.3 102.0 %all-to-all-start = ((f32[8,1,2]{2,1,0:T(1,128)}), f32[8,1,2]{2,1,0:T(1,128)S(1)}, u32[]{:S(2)}, u32[]{:S(2)}) async-start(f32[8,1,2]{2,1,0:T(1,128)} %broadcast_in_dim.8), calls=%async_computation | async-start | bytes 8192 | tf_op jit(solution)/shard_map/all_to_all | solution.py:17
  12.8 10.7 %copy-start.3 = (bf16[6144,256]{0,1:T(8,128)(2,1)S(1)}, bf16[6144,256]{0,1:T(8,128)(2,1)}, u32[]{:S(2)}) copy-start(bf16[6144,256]{0,1:T(8,128)(2,1)} %copy.45) | copy-start | bytes 9437188
  12.8 10.7 %copy-start.13 = (bf16[256,256]{1,0:T(8,128)(2,1)S(1)}, bf16[256,256]{1,0:T(8,128)(2,1)}, u32[]{:S(2)}) copy-start(bf16[256,256]{1,0:T(8,128)(2,1)} %param.24) | copy-start | bytes 393220
  18.2 8.7 %copy-start.2 = (s32[6144]{0:T(1024)S(1)}, s32[6144]{0:T(1024)}, u32[]{:S(2)}) copy-start(s32[6144]{0:T(1024)} %param.21) | copy-start | bytes 73732
  33.7 34.3 %copy-start.7 = (s32[6144]{0:T(1024)}, s32[6144]{0:T(1024)S(1)}, u32[]{:S(2)}) copy-start(s32[6144]{0:T(1024)S(1)} %get-tuple-element.27) | copy-start | bytes 73732
  68.0 47.5 %copy-start.17 = (bf16[16,32]{1,0:T(8,128)(2,1)S(1)}, bf16[16,32]{1,0:T(8,128)(2,1)}, u32[]{:S(2)}) copy-start(bf16[16,32]{1,0:T(8,128)(2,1)} %param.26) | copy-start | bytes 3076
  68.1 47.5 %copy-start.24 = (f32[32]{0:T(128)S(1)}, f32[32]{0:T(128)}, u32[]{:S(2)}) copy-start(f32[32]{0:T(128)} %param.27) | copy-start | bytes 388
  103.3 212.9 %all-to-all-start.2 = ((s32[128,48,2]{1,2,0:T(2,128)}), s32[128,48,2]{1,2,0:T(2,128)}, u32[]{:S(2)}, u32[]{:S(2)}) async-start(s32[128,48,2]{1,2,0:T(2,128)} %copy.52), calls=%async_computation.2 | async-start | bytes 262144 | tf_op jit(solution)/shard_map/all_to_all | solution.py:46
  126.4 9.1 %copy-start.6 = (bf16[6144,256]{0,1:T(8,128)(2,1)S(1)}, bf16[6144,256]{0,1:T(8,128)(2,1)}, u32[]{:S(2)}) copy-start(bf16[6144,256]{0,1:T(8,128)(2,1)} %convolution_convert_fusion.1) | copy-start | bytes 9437188
  126.4 77.4 %copy-start.14 = (f32[16,16]{1,0:T(8,128)S(1)}, f32[16,16]{1,0:T(8,128)}, u32[]{:S(2)}) copy-start(f32[16,16]{1,0:T(8,128)} %param.30) | copy-start | bytes 3076
  126.4 77.7 %copy-start.15 = (f32[16,16]{1,0:T(8,128)S(1)}, f32[16,16]{1,0:T(8,128)}, u32[]{:S(2)}) copy-start(f32[16,16]{1,0:T(8,128)} %param.29) | copy-start | bytes 3076
  126.5 78.1 %copy-start.16 = (f32[16,16]{1,0:T(8,128)S(1)}, f32[16,16]{1,0:T(8,128)}, u32[]{:S(2)}) copy-start(f32[16,16]{1,0:T(8,128)} %param.31) | copy-start | bytes 3076
  135.5 74.2 %copy-start.9 = (bf16[256,256]{1,0:T(8,128)(2,1)S(1)}, bf16[256,256]{1,0:T(8,128)(2,1)}, u32[]{:S(2)}) copy-start(bf16[256,256]{1,0:T(8,128)(2,1)} %param.32) | copy-start | bytes 393220
  135.5 74.2 %copy-start.10 = (f32[256]{0:T(256)S(1)}, f32[256]{0:T(256)}, u32[]{:S(2)}) copy-start(f32[256]{0:T(256)} %param.33) | copy-start | bytes 3076
  203.8 5.9 %copy-start.4 = (bf16[6144,256]{0,1:T(8,128)(2,1)S(1)}, bf16[6144,256]{0,1:T(8,128)(2,1)}, u32[]{:S(2)}) copy-start(bf16[6144,256]{0,1:T(8,128)(2,1)} %copy.45) | copy-start | bytes 9437188
  209.7 4.1 %copy-start.18 = (f32[1024]{0:T(1024)S(1)}, f32[1024]{0:T(1024)}, u32[]{:S(2)}) copy-start(f32[1024]{0:T(1024)} %param.37) | copy-start | bytes 12292
  209.7 4.1 %copy-start.21 = (f32[256]{0:T(256)S(1)}, f32[256]{0:T(256)}, u32[]{:S(2)}) copy-start(f32[256]{0:T(256)} %param.35) | copy-start | bytes 3076
  209.7 4.1 %copy-start.22 = (f32[256]{0:T(256)S(1)}, f32[256]{0:T(256)}, u32[]{:S(2)}) copy-start(f32[256]{0:T(256)} %param.34) | copy-start | bytes 3076
  211.2 2.6 copy-start.5
  213.8 58.6 %copy-start.11 = (bf16[1024,256]{1,0:T(8,128)(2,1)S(1)}, bf16[1024,256]{1,0:T(8,128)(2,1)}, u32[]{:S(2)}) copy-start(bf16[1024,256]{1,0:T(8,128)(2,1)} %param.38) | copy-start | bytes 1572868
  213.8 58.6 %copy-start.23 = (f32[256]{0:T(256)S(1)}, f32[256]{0:T(256)}, u32[]{:S(2)}) copy-start(f32[256]{0:T(256)} %param.39) | copy-start | bytes 3076
  272.4 18.7 %copy-start.8 = (s32[6144]{0:T(1024)S(1)}, s32[6144]{0:T(1024)}, u32[]{:S(2)}) copy-start(s32[6144]{0:T(1024)} %copy-done.7) | copy-start | bytes 73732
  316.2 45.9 %all-to-all-start.1 = ((bf16[128,48,256]{2,1,0:T(8,128)(2,1)}), bf16[128,48,256]{2,1,0:T(8,128)(2,1)}, u32[]{:S(2)}, u32[]{:S(2)}) async-start(bf16[128,48,256]{2,1,0:T(8,128)(2,1)} %bitcast.45), calls=%async_computation.1 | async-start | bytes 6291456 | tf_op jit(solution)/shard_map/all_to_all | solution.py:45
  362.1 25.9 %copy-start.1 = (bf16[256,1024]{1,0:T(8,128)(2,1)S(1)}, bf16[256,1024]{1,0:T(8,128)(2,1)}, u32[]{:S(2)}) copy-start(bf16[256,1024]{1,0:T(8,128)(2,1)} %param.36) | copy-start | bytes 1572868
where the time goes:
time: 396 us; the launch traced here: 388 us
  local copies, waits for them, and re-layouts  133 us (34%)
  matrix products  105 us (27%)
  blocking collectives  63.7 us (16%)
  waiting for transfers between devices  33.4 us (8%)
  other arithmetic  29.4 us (7%)
  starting transfers between devices  22.5 us (6%)
    psum x5, blocking collectives, one_axis_at_a_time(): array = lax.psum(array, axis)  63.7 us
    dot_general x1, matrix products, finish_rows(): jnp.dot(normed_two, perceptron_entry_map, preferred_element_type=jnp.floa...  58.5 us
    gather x1, local copies, waits for them, and re-layouts, body(): inference_placement[ordering]  34.3 us
    gather x1, local copies, waits for them, and re-layouts, body(): anchor[ordering]  34.3 us
    all_to_all x1, waiting for transfers between devices, move_rows(): lax.all_to_all(rows[ordering], HEAD_PTS, split_axis=0, concat_axis=0, til...  33.4 us
    gather x1, local copies, waits for them, and re-layouts, move_rows(): return (arrived[placed], arrived_labels[placed, 1])  25.9 us
    gather x1, local copies, waits for them, and re-layouts, move_rows(): rows[ordering]  25.1 us
    dot_general x1, matrix products, finish_rows(): jnp.dot(inner_act, perceptron_exit_map, preferred_element_type=jnp.float32)  15.5 us
  transfers between devices with their start and end apart: 3, of which 1 were waited for; matrix products, arithmetic and copies ran while one was open for 61% of the time, Pallas kernels for 0%

commit v1 on v0

v1 whole, which is shorter than its diff:
```python
import functools
import math

import jax
import jax.numpy as jnp
from jax import lax
from jax.experimental import pallas as pl
from jax.experimental.pallas import tpu as pltpu
from jax.sharding import PartitionSpec as P

MESH = pl.DeviceIdType.MESH
BF = jnp.bfloat16
F32 = jnp.float32
DEVS = 128
ROWS = 6144
PER = 48
C = 256
HEADS, DH, M = 16, 16, 32
SL = HEADS * M
LOG2E = math.log2(math.e)
HI = lax.Precision.HIGHEST
BLK = 256
BLK2 = 384


def iota(shape, dim):
    return lax.broadcasted_iota(jnp.int32, shape, dim)


def nt(a, b, **kw):
    return lax.dot_general(a, b, (((1,), (1,)), ((), ())), preferred_element_type=F32, **kw)


def tn(a, b, **kw):
    return lax.dot_general(a, b, (((0,), (0,)), ((), ())), preferred_element_type=F32, **kw)


def nn(a, b, **kw):
    return jnp.dot(a, b, preferred_element_type=F32, **kw)


def layer_norm(x, gain, bias):
    mean = jnp.mean(x, axis=-1, keepdims=True)
    c = x - mean
    var = jnp.mean(c * c, axis=-1, keepdims=True)
    return c * lax.rsqrt(var + 1e-05) * gain + bias


def slice_m(shape, dim):
    return (iota(shape, dim) % 256) // 8


def slice_h(shape, dim):
    r = iota(shape, dim)
    return (r // 256) * 8 + r % 8


def head_mask():
    return slice_h((SL, C), 0) == iota((SL, C), 1) // DH


def wide_partition(part):
    cols = (iota((DH, C), 1) % DH == iota((DH, C), 0)).astype(BF)
    z = tn(part, cols).astype(BF)
    pick = (slice_m((SL, M), 0) == iota((SL, M), 1)).astype(BF)
    return jnp.where(head_mask(), nn(pick, z), 0.0).astype(BF)


def offset_rows(off):
    pick = (iota((256, M), 0) // 8 == iota((256, M), 1)).astype(F32)
    return nt(pick, jnp.broadcast_to(off, (128, M)), precision=HI)


def slice_softmax(logit_ref, off_ref, inv_ref, width, emit):
    for hh in range(2):
        inv = inv_ref[hh * 8 : hh * 8 + 8, :]
        for lb in range(width // 128):
            a = logit_ref[hh * 256 : hh * 256 + 256, lb * 128 : lb * 128 + 128]
            a = (a + off_ref[...]).reshape(M, 8, 128) * inv
            e = jnp.exp2(a - jnp.max(a, axis=0))
            sw = e * (1.0 / jnp.sum(e, axis=0))
            emit(hh, lb, sw.reshape(256, 128))


def order_kernel(x_ref, pos_ref, xs_ref, lbl_ref, src, dst, ord_v, ord_s, sem):
    def widen(i, _):
        blk = x_ref[pl.ds(i * 16, 16), :].astype(F32)
        src[pl.ds(i * 32, 16, stride=2), :] = blk[:, :128]
        src[pl.ds(i * 32 + 1, 16, stride=2), :] = blk[:, 128:]
        return 0

    lax.fori_loop(0, ROWS // 16, widen, 0, unroll=4)

    before = (iota((256, 256), 0) < iota((256, 256), 1)).astype(BF)
    tri = jnp.concatenate([before, jnp.ones((256, 128), BF)], axis=1)

    def block(k, carry):
        count, acc = carry
        pos = jnp.concatenate([pos_ref[2 * k], pos_ref[2 * k + 1]], axis=1)
        blk = ((pos >> 11) * 21846) >> 16
        inside = pos - blk * ROWS
        target = (blk & 7) * 16 + (blk >> 3)
        me = k * 256 + iota((1, 256), 1)
        hot = (iota((DEVS, 256), 0) == target).astype(F32)
        hot_b = hot.astype(BF)
        ahead = nn(hot_b, tri)
        full = ahead[:, :256] + jnp.concatenate([count, count], axis=1)
        rank = jnp.sum(hot * full, axis=0, keepdims=True).astype(jnp.int32)
        same = iota((64, 256), 0) == rank
        parts = [inside >> 6, inside & 63, me >> 6, me & 63]
        vals = [jnp.where(same, v.astype(F32), 0.0) for v in parts]
        acc = acc + nt(hot_b, jnp.concatenate(vals, axis=0).astype(BF))
        return count + ahead[:, 256:], acc

    zero = jnp.zeros((DEVS, 128), F32)
    _, acc = lax.fori_loop(
        0, ROWS // 256, block, (zero, jnp.zeros((DEVS, 256), F32)), unroll=4
    )
    acc = acc.astype(jnp.int32)
    label = acc[:, 0:64] * 64 + acc[:, 64:128]
    order = acc[:, 128:192] * 64 + acc[:, 192:256]
    pad = jnp.zeros((DEVS, 64), jnp.int32)
    lbl_ref[...] = jnp.concatenate([label, pad], axis=1).reshape(DEVS, 1, 128)
    ord_v[...] = jnp.concatenate([order, pad], axis=1)
    copy = pltpu.make_async_copy(ord_v, ord_s, sem)
    copy.start()
    copy.wait()

    def gather(t, _):
        for r in range(PER):
            dst[pl.ds(t * 96 + 2 * r, 2), :] = src[pl.ds(ord_s[t, r] * 2, 2), :]
        for q in range(PER // 16):
            left = dst[pl.ds(t * 96 + q * 32, 16, stride=2), :]
            right = dst[pl.ds(t * 96 + q * 32 + 1, 16, stride=2), :]
            xs_ref[pl.ds(t * PER + q * 16, 16), :] = jnp.concatenate(
                [left, right], axis=1
            ).astype(BF)
        return 0

    lax.fori_loop(0, DEVS, gather, 0)


def exchange_kernel(
    xs, lbl, sharp, g1, b1, w_f, w_x, part, off, wq, wk, wv,
    rows_in, lbl_in, sout_ref, inv_ref,
    logit, swt, fx_s, acc, tot, bigp, offs, pay, rs, hd, mine, res, shp,
    row_send, row_recv, lbl_send, lbl_recv, small_send, small_recv, own_sem,
):
    h = lax.axis_index("head")
    p = lax.axis_index("pts")
    me = h * 16 + p
    z0, y0, x0, c0 = h // 2, (p // 8) * 2 + h % 2, (p // 2) % 4, p % 2

    def partner(k):
        k = (k * 53) % 128
        z = (z0 + k // 32) % 4
        y = (y0 + (k // 8) % 4) % 4
        x = (x0 + (k // 2) % 4) % 4
        c = (c0 + k % 2) % 2
        return z * 2 + y % 2, (y // 2) * 8 + x * 2 + c

    bar = pltpu.get_barrier_semaphore()

    def greet(k, _):
        pl.semaphore_signal(bar, inc=1, device_id=partner(k), device_id_type=MESH)
        return 0

    lax.fori_loop(1, DEVS, greet, 0)

    own_rows = pltpu.make_async_copy(xs.at[me], rows_in.at[me], own_sem.at[0])
    own_lbl = pltpu.make_async_copy(lbl.at[me], lbl_in.at[me], own_sem.at[1])
    own_rows.start()
    own_lbl.start()
    bigp[...] = wide_partition(part[...])
    offs[...] = offset_rows(off[...])
    acc[...] = jnp.zeros_like(acc)
    tot[...] = jnp.zeros_like(tot)
    pl.semaphore_wait(bar, DEVS - 1)

    def send_small(src, dst, dev, i):
        return pltpu.make_async_remote_copy(
            src_ref=src, dst_ref=dst, send_sem=small_send.at[i], recv_sem=small_recv.at[i],
            device_id=dev, device_id_type=MESH,
        )

    def send_rows(k, _):
        dev = partner(k)
        to = dev[0] * 16 + dev[1]
        pltpu.make_async_remote_copy(
            src_ref=xs.at[to], dst_ref=rows_in.at[me], send_sem=row_send, recv_sem=row_recv,
            device_id=dev, device_id_type=MESH,
        ).start()
        pltpu.make_async_remote_copy(
            src_ref=lbl.at[to], dst_ref=lbl_in.at[me], send_sem=lbl_send, recv_sem=lbl_recv,
            device_id=dev, device_id_type=MESH,
        ).start()
        return 0

    temps = [
        send_small(sharp, shp.at[h], ((h + i) % 8, p), i - 1) for i in range(1, 8)
    ]
    for t in temps:
        t.start()
    shp[h] = sharp[...]
    lax.fori_loop(1, 9, send_rows, 0)
    for t in temps:
        t.wait()
    inv_ref[...] = LOG2E / jnp.concatenate([shp[i] for i in range(8)], axis=0)

    def pass_one(i, _):
        send_rows(9 + i, 0)
        x = xs_flat(xs, i)
        normed = layer_norm(x.astype(F32), g1[...], b1[...]).astype(BF)
        fx_s[...] = nn(normed, w_f[...]).astype(BF)
        xm = nn(normed, w_x[...]).astype(BF)
        logit[...] = nt(bigp[...], xm)

        def emit(hh, lb, sw):
            tot[hh * 256 : hh * 256 + 256, :] += sw
            swt[hh * 256 : hh * 256 + 256, lb * 128 : lb * 128 + 128] = sw.astype(BF)

        slice_softmax(logit, offs, inv_ref, 384, emit)
        acc[...] += nn(swt[...], fx_s[...])
        return 0

    lax.fori_loop(0, ROWS // 384, pass_one, 0)

    mask = head_mask()

    def fold(a):
        a = jnp.where(mask, a, 0.0)
        return jnp.sum(a[:256].reshape(M, 8, C) + a[256:].reshape(M, 8, C), axis=1)

    numer = fold(acc[...])
    total = fold(jnp.broadcast_to(jnp.sum(tot[...], axis=1, keepdims=True), (SL, C)))
    for i, a in enumerate((numer, total)):
        for rg in range(4):
            for lt in range(2):
                pay[i * 8 + rg * 2 + lt] = a[rg * 8 : rg * 8 + 8, lt * 128 : lt * 128 + 128]
    first = [
        send_small(pay.at[(p + i) % 16], rs.at[p], (h, (p + i) % 16), 6 + i)
        for i in range(1, 16)
    ]
    for t in first:
        t.start()
    rs[p] = pay[p]
    lax.fori_loop(25, 35, send_rows, 0)
    for t in first:
        t.wait()
    mine[...] = jnp.sum(rs[...], axis=0)
    second = [send_small(mine, hd.at[h], ((h + i) % 8, p), 21 + i) for i in range(1, 8)]
    for t in second:
        t.start()
    hd[h] = mine[...]
    lax.fori_loop(35, 45, send_rows, 0)
    for t in second:
        t.wait()
    pay[0] = jnp.sum(hd[...], axis=0)
    third = [
        send_small(pay.at[0], res.at[p], (h, (p + i) % 16), 28 + i) for i in range(1, 16)
    ]
    for t in third:
        t.start()
    res[p] = pay[0]
    lax.fori_loop(45, DEVS, send_rows, 0)
    for t in third:
        t.wait()

    def gathered(i):
        return jnp.concatenate(
            [
                jnp.concatenate([res[i * 8 + rg * 2], res[i * 8 + rg * 2 + 1]], axis=1)
                for rg in range(4)
            ],
            axis=0,
        )

    stok = gathered(0) / (gathered(1) + 1e-05)
    same_head = iota((C, C), 0) // DH == iota((C, C), 1) // DH
    rep = (iota((C, DH), 0) % DH == iota((C, DH), 1)).astype(F32)

    def per_head(w):
        wide = nt(nn(rep, w[...], precision=HI), rep, precision=HI)
        return jnp.where(same_head, wide, 0.0)

    q = nn(stok, per_head(wq), precision=HI)
    k = nn(stok, per_head(wk), precision=HI)
    v = nn(stok, per_head(wv), precision=HI)

    def spread(a):
        a = jnp.broadcast_to(a[:, None, :], (M, 8, C)).reshape(256, C)
        return jnp.where(mask, jnp.concatenate([a, a], axis=0), 0.0)

    score = nt(spread(k), q, precision=HI) * (1.0 / math.sqrt(DH))
    score = score.reshape(2, M, 8, M)
    e = jnp.exp(score - jnp.max(score, axis=1, keepdims=True))
    att = (e / jnp.sum(e, axis=1, keepdims=True)).reshape(SL, M)
    sout = tn(att, spread(v), precision=HI)
    sout_ref[...] = spread(sout).astype(BF)

    own_rows.wait()
    own_lbl.wait()
    n = DEVS - 1
    nbr = partner(1)
    pltpu.make_async_remote_copy(
        src_ref=xs.at[pl.ds(0, n)], dst_ref=rows_in.at[pl.ds(0, n)], send_sem=row_send,
        recv_sem=row_recv, device_id=nbr, device_id_type=MESH,
    ).wait()
    pltpu.make_async_remote_copy(
        src_ref=lbl.at[pl.ds(0, n)], dst_ref=lbl_in.at[pl.ds(0, n)], send_sem=lbl_send,
        recv_sem=lbl_recv, device_id=nbr, device_id_type=MESH,
    ).wait()


def xs_flat(xs, i):
    return xs[pl.ds(i * 8, 8)].reshape(384, C)


def serve_kernel(
    x_ref, lbl_ref, sout_ref, inv_ref, g1, b1, w_x, part, off, w_e, b_e, g2, b2, w_1, b_1,
    w_2, b_2, out_ref, logit, swt, bigp, offs, stage, flat,
):
    bigp[...] = wide_partition(part[...])
    offs[...] = offset_rows(off[...])

    def pass_two(i, _):
        x = x_ref[pl.ds(i * BLK2, BLK2), :].astype(F32)
        normed = layer_norm(x, g1[...], b1[...]).astype(BF)
        xm = nn(normed, w_x[...]).astype(BF)
        logit[...] = nt(bigp[...], xm)

        def emit(hh, lb, sw):
            swt[hh * 256 : hh * 256 + 256, lb * 128 : lb * 128 + 128] = sw.astype(BF)

        slice_softmax(logit, offs, inv_ref, BLK2, emit)
        o = tn(swt[...], sout_ref[...]).astype(BF)
        y = x + nn(o, w_e[...]) + b_e[...]
        z = layer_norm(y, g2[...], b2[...]).astype(BF)
        u = nn(z, w_1[...]) + b_1[...]
        g = (0.5 * u * (1.0 + lax.erf(u * math.sqrt(0.5)))).astype(BF)
        y = y + nn(g, w_2[...]) + b_2[...]
        stage[pl.ds(0, BLK2, stride=2), :] = y[:, :128]
        stage[pl.ds(1, BLK2, stride=2), :] = y[:, 128:]
        for s in range(BLK2 // PER):
            for r in range(PER):
                flat[pl.ds(lbl_ref[i * 8 + s, r] * 2, 2), :] = stage[
                    pl.ds((s * PER + r) * 2, 2), :
                ]
        return 0

    lax.fori_loop(0, ROWS // BLK2, pass_two, 0)

    def narrow(i, _):
        left = flat[pl.ds(i * 32, 16, stride=2), :]
        right = flat[pl.ds(i * 32 + 1, 16, stride=2), :]
        out_ref[pl.ds(i * 16, 16), :] = jnp.concatenate([left, right], axis=1).astype(BF)
        return 0

    lax.fori_loop(0, ROWS // 16, narrow, 0, unroll=4)


VM = pl.BlockSpec(memory_space=pltpu.VMEM)
SM = pl.BlockSpec(memory_space=pltpu.SMEM)
LIMIT = 60 * 1024 * 1024


def order_rows(x, pos):
    return pl.pallas_call(
        order_kernel,
        out_shape=[
            jax.ShapeDtypeStruct((ROWS, C), BF),
            jax.ShapeDtypeStruct((DEVS, 1, 128), jnp.int32),
        ],
        in_specs=[VM] * 2,
        out_specs=[VM] * 2,
        scratch_shapes=[
            pltpu.VMEM((ROWS * 2, 128), F32),
            pltpu.VMEM((ROWS * 2, 128), F32),
            pltpu.VMEM((DEVS, 128), jnp.int32),
            pltpu.SMEM((DEVS, 128), jnp.int32),
            pltpu.SemaphoreType.DMA,
        ],
        compiler_params=pltpu.CompilerParams(vmem_limit_bytes=LIMIT),
        name="order_rows",
    )(x, pos)


def exchange(*args):
    dma = pltpu.SemaphoreType.DMA
    return pl.pallas_call(
        exchange_kernel,
        out_shape=[
            jax.ShapeDtypeStruct((DEVS, PER, C), BF),
            jax.ShapeDtypeStruct((DEVS, 1, 128), jnp.int32),
            jax.ShapeDtypeStruct((SL, C), BF),
            jax.ShapeDtypeStruct((HEADS, 128), F32),
        ],
        in_specs=[VM] * len(args),
        out_specs=[VM] * 4,
        scratch_shapes=[
            pltpu.VMEM((SL, 384), F32),
            pltpu.VMEM((SL, 384), BF),
            pltpu.VMEM((384, C), BF),
            pltpu.VMEM((SL, C), F32),
            pltpu.VMEM((SL, 128), F32),
            pltpu.VMEM((SL, C), BF),
            pltpu.VMEM((256, 128), F32),
            pltpu.VMEM((16, 8, 128), F32),
            pltpu.VMEM((16, 8, 128), F32),
            pltpu.VMEM((8, 8, 128), F32),
            pltpu.VMEM((8, 128), F32),
            pltpu.VMEM((16, 8, 128), F32),
            pltpu.VMEM((8, 2, 128), F32),
            dma, dma, dma, dma, dma((44,)), dma((44,)), dma((2,)),
        ],
        compiler_params=pltpu.CompilerParams(
            vmem_limit_bytes=LIMIT, collective_id=0, has_side_effects=True
        ),
        name="exchange",
    )(*args)


def serve_rows(*args):
    return pl.pallas_call(
        serve_kernel,
        out_shape=jax.ShapeDtypeStruct((ROWS, C), BF),
        in_specs=[VM, SM] + [VM] * (len(args) - 2),
        out_specs=VM,
        scratch_shapes=[
            pltpu.VMEM((SL, BLK2), F32),
            pltpu.VMEM((SL, BLK2), BF),
            pltpu.VMEM((SL, C), BF),
            pltpu.VMEM((256, 128), F32),
            pltpu.VMEM((BLK2 * 2, 128), F32),
            pltpu.VMEM((ROWS * 2, 128), F32),
        ],
        compiler_params=pltpu.CompilerParams(vmem_limit_bytes=LIMIT),
        name="serve_rows",
    )(*args)


def body(
    x, pos, g1, b1, w_f, w_x, part, off, sharp, wq, wk, wv, w_e, b_e, g2, b2, w_1, b_1, w_2, b_2
):
    row = lambda a: a.reshape(1, -1)
    xs, lbl = order_rows(x, pos.reshape(48, 1, 128))
    sharp = jnp.broadcast_to(sharp[:, None], (2, 128))
    rows_in, lbl_in, sout, inv = exchange(
        xs.reshape(DEVS, PER, C), lbl, sharp, row(g1), row(b1), w_f, w_x, part, row(off),
        wq, wk, wv,
    )
    served = serve_rows(
        rows_in.reshape(ROWS, C), lbl_in.reshape(DEVS, 128), sout, inv, row(g1), row(b1), w_x,
        part, row(off), w_e, row(b_e), row(g2), row(b2), w_1, row(b_1), w_2, row(b_2),
    )
    return served[None]


def solution(mesh):
    both = ("head", "pts")
    in_specs = (P(both, None), P(both)) + (P(),) * 6 + (P("head"),) + (P(),) * 11
    return jax.shard_map(
        body, mesh=mesh, in_specs=in_specs, out_specs=P("pts", "head", None), check_vma=False
    )
```

time: 396 us -> 149 us (0.38); the launches traced: 388 us -> 148 us
  Pallas kernels: 0 us -> 147 us
  local copies, waits for them, and re-layouts: 133 us -> 1.32 us
  matrix products: 105 us -> 0 us
  blocking collectives: 63.7 us -> 0 us
  waiting for transfers between devices: 33.4 us -> 0 us
  other arithmetic: 29.4 us -> 0 us
  starting transfers between devices: 22.5 us -> 0 us
    pallas_call x0 -> x3, Pallas kernels: none -> 147 us  [the longest x1 82.3 us: exchange(): pl.pallas_call(exchange_kernel, out_shape=[jax.ShapeDtypeStruct((DEVS, PE...]
    gather x4 -> x0, local copies, waits for them, and re-layouts: 120 us -> none  [the longest x1 34.3 us: body(): inference_placement[ordering]]
    dot_general x12 -> x0, matrix products: 94.4 us -> none  [the longest x1 58.5 us: finish_rows(): jnp.dot(normed_two, perceptron_entry_map, preferred_element_type=jnp.floa...]
    psum x5 -> x0, blocking collectives: 63.7 us -> none  [one_axis_at_a_time(): array = lax.psum(array, axis)]
    all_to_all x3 -> x0, waiting for transfers between devices: 33.4 us -> none  [the longest x1 33.4 us: move_rows(): lax.all_to_all(rows[ordering], HEAD_PTS, split_axis=0, concat_axis=0, til...]
    all_to_all x3 -> x0, starting transfers between devices: 22.5 us -> none  [the longest x1 11 us: move_rows(): lax.all_to_all(labels, HEAD_PTS, split_axis=0, concat_axis=0, tiled=True)]
    reduce_sum x5 -> x0, other arithmetic: 15.1 us -> none  [the longest x1 9.07 us: body(): totals = jnp.sum(coefficient_array, axis=0)]
    sort x2 -> x0, other arithmetic: 13.4 us -> none  [the longest x1 6.73 us: body(): ordering = jnp.argsort(target, stable=True)]
  transfers between devices with their start and end apart: 3 -> 0, of which waited for: 1 -> 0; matrix products, arithmetic and copies ran while one was open for 61% -> 0% of each run, Pallas kernels for 0% -> 0%
where the time goes in v1:
time: 149 us; the launch traced here: 148 us
  Pallas kernels  147 us (99%)
    pallas_call x1, Pallas kernels, exchange(): pl.pallas_call(exchange_kernel, out_shape=[jax.ShapeDtypeStruct((DEVS, PE...  82.3 us
    pallas_call x1, Pallas kernels, serve_rows(): pl.pallas_call(serve_kernel, out_shape=jax.ShapeDtypeStruct((ROWS, C), BF...  46.6 us
    pallas_call x1, Pallas kernels, order_rows(): pl.pallas_call(order_kernel, out_shape=[jax.ShapeDtypeStruct((ROWS, C), B...  17.7 us

profile of v1, /device:TPU:1, one launch (start us, length us, event | category | flops | bytes accessed | tf_op | source)
XLA Modules:
  0.0 147.9 jit_solution(17966052378782930592)
XLA Ops:
  0.0 1.3 broadcast_in_dim.4.sharp
  1.3 17.7 %order_rows.1 = (bf16[6144,256]{1,0:T(8,128)(2,1)}, s32[128,1,128]{2,1,0:T(1,128)}) custom-call(bf16[6144,256]{1,0:T(8,128)(2,1)} %x_ref.1, s32[48,1,128]{2,1,0:T(1,128)} %bitcast.16), custom_call_target="tpu_custom_call" | custom-call | tf_op jit(solution)/shard_map/order_rows/pallas_call | solution.py:368
  19.0 82.3 %exchange.1 = (bf16[128,48,256]{2,1,0:T(8,128)(2,1)}, s32[128,1,128]{2,1,0:T(1,128)}, bf16[512,256]{1,0:T(8,128)(2,1)}, f32[16,128]{1,0:T(8,128)}) custom-call(bf16[128,48,256]{2,1,0:T(8,128)(2,1)} %bitcast.13, s32[128,1,128]{2,1,0:T(1,128)} %get-tuple-element.12.lbl, f32[2,128]{1,0:T(2,128)} %broadcast_in_dim.4.sharp, f32[1,256]{1,0:T(1,128)} %bitcast.17, ...), custom_call_target="tpu_custom_call" | custom-call | tf_op jit(solution)/shard_map/exchange/pallas_call | solution.py:390
  101.3 46.6 %serve_rows.1 = bf16[6144,256]{1,0:T(8,128)(2,1)} custom-call(bf16[6144,256]{1,0:T(8,128)(2,1)} %bitcast.14, s32[128,128]{1,0:T(8,128)} %bitcast.15, bf16[512,256]{1,0:T(8,128)(2,1)} %get-tuple-element.15.sout_ref, f32[16,128]{1,0:T(8,128)} %get-tuple-element.16.inv_ref, f32[1,256]{1,0:T(1,128)} %bitcast.18, f32[1,256]{1,0:T(1,128)} %bitcast.20, ...), custom_call_target="tpu_custom_call" | custom-call | tf_op jit(solution)/shard_map/serve_rows/pallas_call | solution.py:424

commit v2 on v1

v2 whole, which is shorter than its diff:
```python
import functools
import math

import jax
import jax.numpy as jnp
from jax import lax
from jax.experimental import pallas as pl
from jax.experimental.pallas import tpu as pltpu
from jax.sharding import PartitionSpec as P

MESH = pl.DeviceIdType.MESH
BF = jnp.bfloat16
F32 = jnp.float32
DEVS = 128
ROWS = 6144
PER = 48
C = 256
HEADS, DH, M = 16, 16, 32
SL = HEADS * M
LOG2E = math.log2(math.e)
HI = lax.Precision.HIGHEST
BLK = 768


def iota(shape, dim):
    return lax.broadcasted_iota(jnp.int32, shape, dim)


def nt(a, b, **kw):
    return lax.dot_general(a, b, (((1,), (1,)), ((), ())), preferred_element_type=F32, **kw)


def tn(a, b, **kw):
    return lax.dot_general(a, b, (((0,), (0,)), ((), ())), preferred_element_type=F32, **kw)


def nn(a, b, **kw):
    return jnp.dot(a, b, preferred_element_type=F32, **kw)


def layer_norm(x, gain, bias):
    mean = jnp.mean(x, axis=-1, keepdims=True)
    c = x - mean
    var = jnp.mean(c * c, axis=-1, keepdims=True)
    return c * lax.rsqrt(var + 1e-05) * gain + bias


def slice_m(shape, dim):
    return (iota(shape, dim) % 256) // 8


def slice_h(shape, dim):
    r = iota(shape, dim)
    return (r // 256) * 8 + r % 8


def head_mask():
    return slice_h((SL, C), 0) == iota((SL, C), 1) // DH


def wide_partition(part):
    cols = (iota((DH, C), 1) % DH == iota((DH, C), 0)).astype(BF)
    z = tn(part, cols).astype(BF)
    pick = (slice_m((SL, M), 0) == iota((SL, M), 1)).astype(BF)
    return jnp.where(head_mask(), nn(pick, z), 0.0).astype(BF)


def offset_rows(off):
    pick = (iota((256, M), 0) // 8 == iota((256, M), 1)).astype(F32)
    return nt(pick, jnp.broadcast_to(off, (128, M)), precision=HI)


def slice_softmax(logit_ref, off_ref, inv_ref, width, emit):
    for hh in range(2):
        inv = inv_ref[hh * 8 : hh * 8 + 8, :]
        for lb in range(width // 128):
            a = logit_ref[hh * 256 : hh * 256 + 256, lb * 128 : lb * 128 + 128]
            a = (a + off_ref[...]).reshape(M, 8, 128) * inv
            e = jnp.exp2(a - jnp.max(a, axis=0))
            sw = e * (1.0 / jnp.sum(e, axis=0))
            emit(hh, lb, sw.reshape(256, 128))


def exchange_kernel(
    x_hbm, pos_ref, sharp, g1, b1, w_f, w_x, part, off, wq, wk, wv, w_e, b_e, g2, b2, w_1, b_1,
    w_2, b_2, y_hbm, lbl_in,
    xv, src, hop, xsend, rows_in, lbl, ord_v, ord_s, logit, swt, fx_s, acc, tot, bigp, offs,
    wide, pay, rs, hd, mine, res, shp, inv_ref, sout_ref, stage,
    x_sem, ord_sem, y_sem, row_send, row_recv, lbl_send, lbl_recv, small_send, small_recv,
):
    h = lax.axis_index("head")
    p = lax.axis_index("pts")
    z0, y0, x0, c0 = h // 2, (p // 8) * 2 + h % 2, (p // 2) % 4, p % 2

    def partner(k):
        k = (k * 53) % 128
        z = (z0 + k // 32) % 4
        y = (y0 + (k // 8) % 4) % 4
        x = (x0 + (k // 2) % 4) % 4
        c = (c0 + k % 2) % 2
        return z * 2 + y % 2, (y // 2) * 8 + x * 2 + c

    load_x = pltpu.make_async_copy(x_hbm, xv, x_sem)
    load_x.start()
    bar = pltpu.get_barrier_semaphore()

    def greet(k, _):
        pl.semaphore_signal(bar, inc=1, device_id=partner(k), device_id_type=MESH)
        return 0

    lax.fori_loop(1, DEVS, greet, 0)

    before = (iota((256, 256), 0) < iota((256, 256), 1)).astype(BF)
    tri = jnp.concatenate([before, jnp.ones((256, 128), BF)], axis=1)

    def block(k, carry):
        count, total = carry
        pos = jnp.concatenate([pos_ref[2 * k], pos_ref[2 * k + 1]], axis=1)
        blk = ((pos >> 11) * 21846) >> 16
        inside = pos - blk * ROWS
        target = (blk & 7) * 16 + (blk >> 3)
        me = k * 256 + iota((1, 256), 1)
        hot = (iota((DEVS, 256), 0) == target).astype(F32)
        hot_b = hot.astype(BF)
        ahead = nn(hot_b, tri)
        full = ahead[:, :256] + jnp.concatenate([count, count], axis=1)
        rank = jnp.sum(hot * full, axis=0, keepdims=True).astype(jnp.int32)
        same = iota((64, 256), 0) == rank
        parts = [inside >> 6, inside & 63, me >> 6, me & 63]
        vals = [jnp.where(same, v.astype(F32), 0.0) for v in parts]
        total = total + nt(hot_b, jnp.concatenate(vals, axis=0).astype(BF))
        return count + ahead[:, 256:], total

    zero = jnp.zeros((DEVS, 128), F32)
    _, order = lax.fori_loop(
        0, ROWS // 256, block, (zero, jnp.zeros((DEVS, 256), F32)), unroll=4
    )
    order = order.astype(jnp.int32)
    pad = jnp.zeros((DEVS, 64), jnp.int32)
    label = order[:, 0:64] * 64 + order[:, 64:128]
    lbl[...] = jnp.concatenate([label * 2, pad], axis=1).reshape(DEVS, 1, 128)
    order = order[:, 128:192] * 64 + order[:, 192:256]
    order = jnp.clip(order * 2, 0, ROWS * 2 - 2)
    ord_v[...] = jnp.concatenate([order, pad], axis=1)
    save_order = pltpu.make_async_copy(ord_v, ord_s, ord_sem)
    save_order.start()
    load_x.wait()

    def widen(i, _):
        blk = xv[pl.ds(i * 16, 16), :].astype(F32)
        src[pl.ds(i * 32, 16, stride=2), :] = blk[:, :128]
        src[pl.ds(i * 32 + 1, 16, stride=2), :] = blk[:, 128:]
        return 0

    lax.fori_loop(0, ROWS // 16, widen, 0, unroll=8)
    save_order.wait()

    def gather(k, _):
        dev = partner(k)
        to = dev[0] * 16 + dev[1]
        for r in range(PER):
            hop[2 * r : 2 * r + 2, :] = src[pl.ds(ord_s[to, r], 2), :]
        for q in range(PER // 16):
            left = hop[pl.ds(q * 32, 16, stride=2), :]
            right = hop[pl.ds(q * 32 + 1, 16, stride=2), :]
            both = jnp.concatenate([left, right], axis=1).astype(BF)
            xsend[k, q * 16 : q * 16 + 16, :] = both
        return 0

    lax.fori_loop(0, 9, gather, 0)
    rows_in[0] = xsend[0]
    lbl_in[0] = lbl[h * 16 + p]

    bigp[...] = wide_partition(part[...])
    offs[...] = offset_rows(off[...])
    same_head = iota((C, C), 0) // DH == iota((C, C), 1) // DH
    rep = (iota((C, DH), 0) % DH == iota((C, DH), 1)).astype(F32)
    for i, w in enumerate((wq, wk, wv)):
        full = nt(nn(rep, w[...], precision=HI), rep, precision=HI)
        wide[i] = jnp.where(same_head, full, 0.0)
    acc[...] = jnp.zeros_like(acc)
    tot[...] = jnp.zeros_like(tot)
    pl.semaphore_wait(bar, DEVS - 1)

    def send_small(src, dst, dev, i):
        return pltpu.make_async_remote_copy(
            src_ref=src, dst_ref=dst, send_sem=small_send.at[i], recv_sem=small_recv.at[i],
            device_id=dev, device_id_type=MESH,
        )

    def send_rows(k, _):
        dev = partner(k)
        to = dev[0] * 16 + dev[1]
        pltpu.make_async_remote_copy(
            src_ref=xsend.at[k], dst_ref=rows_in.at[k], send_sem=row_send,
            recv_sem=row_recv.at[k // 16], device_id=dev, device_id_type=MESH,
        ).start()
        pltpu.make_async_remote_copy(
            src_ref=lbl.at[to], dst_ref=lbl_in.at[k], send_sem=lbl_send, recv_sem=lbl_recv,
            device_id=dev, device_id_type=MESH,
        ).start()
        return 0

    def move(first, count, ahead):
        lax.fori_loop(first, first + count, send_rows, 0)
        lax.fori_loop(first + count, first + count + ahead, gather, 0)

    temps = [send_small(sharp, shp.at[h], ((h + i) % 8, p), i - 1) for i in range(1, 8)]
    for t in temps:
        t.start()
    shp[h] = sharp[...]
    move(1, 8, 6)
    for t in temps:
        t.wait()
    inv_ref[...] = LOG2E / jnp.concatenate([shp[i] for i in range(8)], axis=0)

    def pass_one(i, _):
        move(9 + 6 * i, 6, 6)
        normed = layer_norm(xv[pl.ds(i * BLK, BLK), :].astype(F32), g1[...], b1[...]).astype(BF)
        fx_s[...] = nn(normed, w_f[...]).astype(BF)
        xm = nn(normed, w_x[...]).astype(BF)
        logit[...] = nt(bigp[...], xm)

        def emit(hh, lb, sw):
            tot[hh * 256 : hh * 256 + 256, :] += sw
            swt[hh * 256 : hh * 256 + 256, lb * 128 : lb * 128 + 128] = sw.astype(BF)

        slice_softmax(logit, offs, inv_ref, BLK, emit)
        acc[...] += nn(swt[...], fx_s[...])
        return 0

    lax.fori_loop(0, ROWS // BLK, pass_one, 0)

    mask = head_mask()

    def fold(a):
        a = jnp.where(mask, a, 0.0)
        return jnp.sum(a[:256].reshape(M, 8, C) + a[256:].reshape(M, 8, C), axis=1)

    numer = fold(acc[...])
    total = fold(jnp.broadcast_to(jnp.sum(tot[...], axis=1, keepdims=True), (SL, C)))
    for i, a in enumerate((numer, total)):
        for rg in range(4):
            for lt in range(2):
                pay[i * 8 + rg * 2 + lt] = a[rg * 8 : rg * 8 + 8, lt * 128 : lt * 128 + 128]
    first = [
        send_small(pay.at[(p + i) % 16], rs.at[p], (h, (p + i) % 16), 6 + i)
        for i in range(1, 16)
    ]
    for t in first:
        t.start()
    rs[p] = pay[p]
    move(57, 6, 10)
    for t in first:
        t.wait()
    mine[...] = jnp.sum(rs[...], axis=0)
    second = [send_small(mine, hd.at[h], ((h + i) % 8, p), 21 + i) for i in range(1, 8)]
    for t in second:
        t.start()
    hd[h] = mine[...]
    move(63, 10, 10)
    for t in second:
        t.wait()
    pay[0] = jnp.sum(hd[...], axis=0)
    third = [
        send_small(pay.at[0], res.at[p], (h, (p + i) % 16), 28 + i) for i in range(1, 16)
    ]
    for t in third:
        t.start()
    res[p] = pay[0]
    move(73, 10, 45)
    lax.fori_loop(83, DEVS, send_rows, 0)
    for t in third:
        t.wait()

    def gathered(i):
        return jnp.concatenate(
            [
                jnp.concatenate([res[i * 8 + rg * 2], res[i * 8 + rg * 2 + 1]], axis=1)
                for rg in range(4)
            ],
            axis=0,
        )

    stok = gathered(0) / (gathered(1) + 1e-05)
    q, k, v = (nn(stok, wide[i], precision=HI) for i in range(3))

    def spread(a):
        a = jnp.broadcast_to(a[:, None, :], (M, 8, C)).reshape(256, C)
        return jnp.where(mask, jnp.concatenate([a, a], axis=0), 0.0)

    score = nt(spread(k), q, precision=HI) * (1.0 / math.sqrt(DH))
    score = score.reshape(2, M, 8, M)
    e = jnp.exp(score - jnp.max(score, axis=1, keepdims=True))
    att = (e / jnp.sum(e, axis=1, keepdims=True)).reshape(SL, M)
    sout = tn(att, spread(v), precision=HI)
    sout_ref[...] = spread(sout).astype(BF)

    nbr = partner(1)

    def arrived(n, sem):
        pltpu.make_async_remote_copy(
            src_ref=xsend.at[pl.ds(0, n)], dst_ref=rows_in.at[pl.ds(0, n)], send_sem=row_send,
            recv_sem=sem, device_id=nbr, device_id_type=MESH,
        ).wait_recv()

    def pass_two(i, _):
        @pl.when(i == 0)
        def _():
            arrived(15, row_recv.at[0])

        @pl.when(i > 0)
        def _():
            arrived(16, row_recv.at[i])

        x = rows_in[pl.ds(i * 16, 16)].reshape(BLK, C).astype(F32)
        normed = layer_norm(x, g1[...], b1[...]).astype(BF)
        xm = nn(normed, w_x[...]).astype(BF)
        logit[...] = nt(bigp[...], xm)

        def emit(hh, lb, sw):
            swt[hh * 256 : hh * 256 + 256, lb * 128 : lb * 128 + 128] = sw.astype(BF)

        slice_softmax(logit, offs, inv_ref, BLK, emit)
        o = tn(swt[...], sout_ref[...]).astype(BF)
        y = x + nn(o, w_e[...]) + b_e[...]
        z = layer_norm(y, g2[...], b2[...]).astype(BF)
        u = nn(z, w_1[...]) + b_1[...]
        g = (u * (1.0 + lax.erf(u * math.sqrt(0.5)))).astype(BF)
        y = y + 0.5 * nn(g, w_2[...]) + b_2[...]
        at = i * BLK * 2
        stage[pl.ds(at, BLK, stride=2), :] = y[:, :128]
        stage[pl.ds(at + 1, BLK, stride=2), :] = y[:, 128:]
        rows = pl.ds(at, BLK * 2)
        pltpu.make_async_copy(stage.at[rows], y_hbm.at[rows], y_sem.at[i]).start()
        return 0

    lax.fori_loop(0, ROWS // BLK, pass_two, 0)

    n = DEVS - 1
    pltpu.make_async_remote_copy(
        src_ref=xsend.at[pl.ds(0, n)], dst_ref=rows_in.at[pl.ds(0, n)], send_sem=row_send,
        recv_sem=row_recv.at[0], device_id=nbr, device_id_type=MESH,
    ).wait_send()
    pltpu.make_async_remote_copy(
        src_ref=lbl.at[pl.ds(0, n)], dst_ref=lbl_in.at[pl.ds(0, n)], send_sem=lbl_send,
        recv_sem=lbl_recv, device_id=nbr, device_id_type=MESH,
    ).wait()
    for i in range(ROWS // BLK):
        rows = pl.ds(i * BLK * 2, BLK * 2)
        pltpu.make_async_copy(stage.at[rows], y_hbm.at[rows], y_sem.at[i]).wait()


PIECES = 8


def place_kernel(y_hbm, lbl_ref, out_hbm, y, flat, out_v, in_sem, out_sem):
    size = ROWS * 2 // PIECES
    loads = []
    for i in range(PIECES):
        rows = pl.ds(i * size, size)
        loads.append(pltpu.make_async_copy(y_hbm.at[rows], y.at[rows], in_sem.at[i]))
        loads[-1].start()

    def scatter(t, _):
        for r in range(PER):
            flat[pl.ds(lbl_ref[t, r], 2), :] = y[pl.ds(t * PER * 2 + 2 * r, 2), :]
        return 0

    for i in range(PIECES):
        loads[i].wait()
        lax.fori_loop(i * DEVS // PIECES, (i + 1) * DEVS // PIECES, scatter, 0, unroll=2)

    def narrow(i, _):
        left = flat[pl.ds(i * 32, 16, stride=2), :]
        right = flat[pl.ds(i * 32 + 1, 16, stride=2), :]
        out_v[pl.ds(i * 16, 16), :] = jnp.concatenate([left, right], axis=1).astype(BF)
        return 0

    stores = []
    for i in range(PIECES):
        lo, hi = i * ROWS // PIECES, (i + 1) * ROWS // PIECES
        lax.fori_loop(lo // 16, hi // 16, narrow, 0, unroll=8)
        rows = pl.ds(lo, hi - lo)
        stores.append(pltpu.make_async_copy(out_v.at[rows], out_hbm.at[rows], out_sem.at[i]))
        stores[-1].start()
    for s in stores:
        s.wait()


VM = pl.BlockSpec(memory_space=pltpu.VMEM)
SM = pl.BlockSpec(memory_space=pltpu.SMEM)
ANY = pl.BlockSpec(memory_space=pl.ANY)
LIMIT = 60 * 1024 * 1024


def exchange(*args):
    dma = pltpu.SemaphoreType.DMA
    return pl.pallas_call(
        exchange_kernel,
        out_shape=[
            jax.ShapeDtypeStruct((ROWS * 2, 128), F32),
            jax.ShapeDtypeStruct((DEVS, 1, 128), jnp.int32),
        ],
        in_specs=[ANY] + [VM] * (len(args) - 1),
        out_specs=[ANY, VM],
        scratch_shapes=[
            pltpu.VMEM((ROWS, C), BF),
            pltpu.VMEM((ROWS * 2, 128), F32),
            pltpu.VMEM((PER * 2, 128), F32),
            pltpu.VMEM((DEVS, PER, C), BF),
            pltpu.VMEM((DEVS, PER, C), BF),
            pltpu.VMEM((DEVS, 1, 128), jnp.int32),
            pltpu.VMEM((DEVS, 128), jnp.int32),
            pltpu.SMEM((DEVS, 128), jnp.int32),
            pltpu.VMEM((SL, BLK), F32),
            pltpu.VMEM((SL, BLK), BF),
            pltpu.VMEM((BLK, C), BF),
            pltpu.VMEM((SL, C), F32),
            pltpu.VMEM((SL, 128), F32),
            pltpu.VMEM((SL, C), BF),
            pltpu.VMEM((256, 128), F32),
            pltpu.VMEM((3, C, C), F32),
            pltpu.VMEM((16, 8, 128), F32),
            pltpu.VMEM((16, 8, 128), F32),
            pltpu.VMEM((8, 8, 128), F32),
            pltpu.VMEM((8, 128), F32),
            pltpu.VMEM((16, 8, 128), F32),
            pltpu.VMEM((8, 2, 128), F32),
            pltpu.VMEM((HEADS, 128), F32),
            pltpu.VMEM((SL, C), BF),
            pltpu.VMEM((ROWS * 2, 128), F32),
            dma, dma, dma((ROWS // BLK,)), dma, dma((8,)), dma, dma, dma((44,)), dma((44,)),
        ],
        compiler_params=pltpu.CompilerParams(
            vmem_limit_bytes=LIMIT, collective_id=0, has_side_effects=True
        ),
        name="exchange",
    )(*args)


def place_rows(y, lbl):
    return pl.pallas_call(
        place_kernel,
        out_shape=jax.ShapeDtypeStruct((ROWS, C), BF),
        in_specs=[ANY, SM],
        out_specs=ANY,
        scratch_shapes=[
            pltpu.VMEM((ROWS * 2, 128), F32),
            pltpu.VMEM((ROWS * 2, 128), F32),
            pltpu.VMEM((ROWS, C), BF),
            pltpu.SemaphoreType.DMA((PIECES,)),
            pltpu.SemaphoreType.DMA((PIECES,)),
        ],
        compiler_params=pltpu.CompilerParams(vmem_limit_bytes=LIMIT),
        name="place_rows",
    )(y, lbl)


def body(
    x, pos, g1, b1, w_f, w_x, part, off, sharp, wq, wk, wv, w_e, b_e, g2, b2, w_1, b_1, w_2, b_2
):
    row = lambda a: a.reshape(1, -1)
    y, lbl = exchange(
        x, pos.reshape(48, 1, 128), jnp.broadcast_to(sharp[:, None], (2, 128)), row(g1),
        row(b1), w_f, w_x, part, row(off), wq, wk, wv, w_e, row(b_e), row(g2), row(b2), w_1,
        row(b_1), w_2, row(b_2),
    )
    return place_rows(y, lbl.reshape(DEVS, 128))[None]


def solution(mesh):
    both = ("head", "pts")
    in_specs = (P(both, None), P(both)) + (P(),) * 6 + (P("head"),) + (P(),) * 11
    return jax.shard_map(
        body, mesh=mesh, in_specs=in_specs, out_specs=P("pts", "head", None), check_vma=False
    )
```

time: 149 us -> 106 us (0.71)
  Pallas kernels: 147 us -> 105 us
    pallas_call x3 -> x2, Pallas kernels: 147 us -> 105 us  [the longest x1 94.7 us: exchange(): pl.pallas_call(exchange_kernel, out_shape=[jax.ShapeDtypeStruct((ROWS * 2...]
where the time goes in v2:
time: 106 us
  Pallas kernels  105 us (99%)
  local copies, waits for them, and re-layouts  1.28 us (1%)
    pallas_call x1, Pallas kernels, exchange(): pl.pallas_call(exchange_kernel, out_shape=[jax.ShapeDtypeStruct((ROWS * 2...  94.7 us
    pallas_call x1, Pallas kernels, place_rows(): pl.pallas_call(place_kernel, out_shape=jax.ShapeDtypeStruct((ROWS, C), BF...  9.9 us

profile of v2, /device:TPU:1, one launch (start us, length us, event | category | flops | bytes accessed | tf_op | source)
XLA Modules:
  0.0 105.9 jit_solution(338857710025093669)
XLA Ops:
  0.0 1.3 %broadcast_in_dim.4.sharp = f32[2,128]{1,0:T(2,128)} broadcast(f32[2]{0:T(128)} %param.28), dimensions={0} | broadcast | bytes 1032 | tf_op jit(solution)/shard_map/broadcast_in_dim | solution.py:465
  1.3 94.7 %exchange.1 = (f32[12288,128]{1,0:T(8,128)}, s32[128,1,128]{2,1,0:T(1,128)}) custom-call(bf16[6144,256]{1,0:T(8,128)(2,1)} %x_hbm.1, s32[48,1,128]{2,1,0:T(1,128)} %bitcast.12, f32[2,128]{1,0:T(2,128)} %broadcast_in_dim.4.sharp, f32[1,256]{1,0:T(1,128)} %bitcast.14, f32[1,256]{1,0:T(1,128)} %bitcast.15, bf16[256,256]{1,0:T(8,128)(2,1)} %w_f.1, ...), custom_call_target="tpu_custom_call" | custom-call | tf_op jit(solution)/shard_map/exchange/pallas_call | solution.py:399
  96.0 9.9 %place_rows.1 = bf16[6144,256]{1,0:T(8,128)(2,1)} custom-call(f32[12288,128]{1,0:T(8,128)} %get-tuple-element.7.y_hbm, s32[128,128]{1,0:T(8,128)} %bitcast.11), custom_call_target="tpu_custom_call" | custom-call | tf_op jit(solution)/shard_map/place_rows/pallas_call | solution.py:443

commit v3 on v2

--- a/solution.py
+++ b/solution.py
@@ -20,6 +20,9 @@
 LOG2E = math.log2(math.e)
 HI = lax.Precision.HIGHEST
 BLK = 768
+SUB = 256
+FSUB = 384
+EARLY = 6
 
 
 def iota(shape, dim):
@@ -70,10 +73,17 @@
     return nt(pick, jnp.broadcast_to(off, (128, M)), precision=HI)
 
 
-def slice_softmax(logit_ref, off_ref, inv_ref, width, emit):
+def skewed(count, *stages):
+    for step in range(count + len(stages) - 1):
+        for t in reversed(range(len(stages))):
+            if 0 <= step - t < count:
+                stages[t](step - t)
+
+
+def slice_softmax(logit_ref, off_ref, inv_ref, lanes, emit):
     for hh in range(2):
         inv = inv_ref[hh * 8 : hh * 8 + 8, :]
-        for lb in range(width // 128):
+        for lb in lanes:
             a = logit_ref[hh * 256 : hh * 256 + 256, lb * 128 : lb * 128 + 128]
             a = (a + off_ref[...]).reshape(M, 8, 128) * inv
             e = jnp.exp2(a - jnp.max(a, axis=0))
@@ -81,34 +91,40 @@
             emit(hh, lb, sw.reshape(256, 128))
 
 
+def sub_lanes(s):
+    return range(s * SUB // 128, (s + 1) * SUB // 128)
+
+
 def exchange_kernel(
     x_hbm, pos_ref, sharp, g1, b1, w_f, w_x, part, off, wq, wk, wv, w_e, b_e, g2, b2, w_1, b_1,
     w_2, b_2, y_hbm, lbl_in,
     xv, src, hop, xsend, rows_in, lbl, ord_v, ord_s, logit, swt, fx_s, acc, tot, bigp, offs,
-    wide, pay, rs, hd, mine, res, shp, inv_ref, sout_ref, stage,
+    wide, pay, rs, hd, mine, res, own_temp, shp, inv_ref, sout_ref, stage,
     x_sem, ord_sem, y_sem, row_send, row_recv, lbl_send, lbl_recv, small_send, small_recv,
 ):
     h = lax.axis_index("head")
     p = lax.axis_index("pts")
-    z0, y0, x0, c0 = h // 2, (p // 8) * 2 + h % 2, (p // 2) % 4, p % 2
+    z0, y0, x0, c0 = h >> 1, ((p >> 3) << 1) + (h & 1), (p >> 1) & 3, p & 1
 
     def partner(k):
-        k = (k * 53) % 128
-        z = (z0 + k // 32) % 4
-        y = (y0 + (k // 8) % 4) % 4
-        x = (x0 + (k // 2) % 4) % 4
-        c = (c0 + k % 2) % 2
-        return z * 2 + y % 2, (y // 2) * 8 + x * 2 + c
+        k = (k * 53) & 127
+        z = (z0 + (k >> 5)) & 3
+        y = (y0 + (k >> 3)) & 3
+        x = (x0 + (k >> 1)) & 3
+        c = (c0 + k) & 1
+        return z * 2 + (y & 1), (y >> 1) * 8 + x * 2 + c
 
     load_x = pltpu.make_async_copy(x_hbm, xv, x_sem)
     load_x.start()
+    both = [jnp.full((1, 128), sharp[i], F32) for i in range(2)]
+    own_temp[...] = jnp.concatenate(both, axis=0)
     bar = pltpu.get_barrier_semaphore()
 
     def greet(k, _):
         pl.semaphore_signal(bar, inc=1, device_id=partner(k), device_id_type=MESH)
         return 0
 
-    lax.fori_loop(1, DEVS, greet, 0)
+    lax.fori_loop(1, DEVS, greet, 0, unroll=4)
 
     before = (iota((256, 256), 0) < iota((256, 256), 1)).astype(BF)
     tri = jnp.concatenate([before, jnp.ones((256, 128), BF)], axis=1)
@@ -144,42 +160,6 @@
     ord_v[...] = jnp.concatenate([order, pad], axis=1)
     save_order = pltpu.make_async_copy(ord_v, ord_s, ord_sem)
     save_order.start()
-    load_x.wait()
-
-    def widen(i, _):
-        blk = xv[pl.ds(i * 16, 16), :].astype(F32)
-        src[pl.ds(i * 32, 16, stride=2), :] = blk[:, :128]
-        src[pl.ds(i * 32 + 1, 16, stride=2), :] = blk[:, 128:]
-        return 0
-
-    lax.fori_loop(0, ROWS // 16, widen, 0, unroll=8)
-    save_order.wait()
-
-    def gather(k, _):
-        dev = partner(k)
-        to = dev[0] * 16 + dev[1]
-        for r in range(PER):
-            hop[2 * r : 2 * r + 2, :] = src[pl.ds(ord_s[to, r], 2), :]
-        for q in range(PER // 16):
-            left = hop[pl.ds(q * 32, 16, stride=2), :]
-            right = hop[pl.ds(q * 32 + 1, 16, stride=2), :]
-            both = jnp.concatenate([left, right], axis=1).astype(BF)
-            xsend[k, q * 16 : q * 16 + 16, :] = both
-        return 0
-
-    lax.fori_loop(0, 9, gather, 0)
-    rows_in[0] = xsend[0]
-    lbl_in[0] = lbl[h * 16 + p]
-
-    bigp[...] = wide_partition(part[...])
-    offs[...] = offset_rows(off[...])
-    same_head = iota((C, C), 0) // DH == iota((C, C), 1) // DH
-    rep = (iota((C, DH), 0) % DH == iota((C, DH), 1)).astype(F32)
-    for i, w in enumerate((wq, wk, wv)):
-        full = nt(nn(rep, w[...], precision=HI), rep, precision=HI)
-        wide[i] = jnp.where(same_head, full, 0.0)
-    acc[...] = jnp.zeros_like(acc)
-    tot[...] = jnp.zeros_like(tot)
     pl.semaphore_wait(bar, DEVS - 1)
 
     def send_small(src, dst, dev, i):
@@ -201,35 +181,130 @@
         ).start()
         return 0
 
-    def move(first, count, ahead):
-        lax.fori_loop(first, first + count, send_rows, 0)
-        lax.fori_loop(first + count, first + count + ahead, gather, 0)
-
-    temps = [send_small(sharp, shp.at[h], ((h + i) % 8, p), i - 1) for i in range(1, 8)]
+    def send(first, stop):
+        lax.fori_loop(first, stop, send_rows, 0)
+
+    shp[h] = own_temp[...]
+    temps = [send_small(own_temp, shp.at[h], ((h + i) % 8, p), i - 1) for i in range(1, 8)]
     for t in temps:
         t.start()
-    shp[h] = sharp[...]
-    move(1, 8, 6)
+    load_x.wait()
+
+    def widen(i, _):
+        blk = xv[pl.ds(i * 16, 16), :].astype(F32)
+        src[pl.ds(i * 32, 16, stride=2), :] = blk[:, :128]
+        src[pl.ds(i * 32 + 1, 16, stride=2), :] = blk[:, 128:]
+        return 0
+
+    lax.fori_loop(0, ROWS // 16, widen, 0, unroll=8)
+    save_order.wait()
+
+    def gather(first, count):
+        for i in range(count):
+            dev = partner(first + i)
+            picks = ord_s.at[dev[0] * 16 + dev[1]]
+            for r in range(PER):
+                at = (i * PER + r) * 2
+                hop[at : at + 2, :] = src[pl.ds(picks[r], 2), :]
+            for q in range(PER // 16):
+                at = i * PER * 2 + q * 32
+                left = hop[pl.ds(at, 16, stride=2), :]
+                right = hop[pl.ds(at + 1, 16, stride=2), :]
+                both = jnp.concatenate([left, right], axis=1).astype(BF)
+                xsend[first + i, q * 16 : q * 16 + 16, :] = both
+
+    gather(0, 16)
+    rows_in[0] = xsend[0]
+    lbl_in[0] = lbl[h * 16 + p]
+
+    send(1, 7)
+    bigp[...] = wide_partition(part[...])
+    offs[...] = offset_rows(off[...])
+    same_head = iota((C, C), 0) // DH == iota((C, C), 1) // DH
+    rep = (iota((C, DH), 0) % DH == iota((C, DH), 1)).astype(F32)
+    for i, w in enumerate((wq, wk, wv)):
+        full = nt(nn(rep, w[...], precision=HI), rep, precision=HI)
+        wide[i] = jnp.where(same_head, full, 0.0)
+    acc[...] = jnp.zeros_like(acc)
+    tot[...] = jnp.zeros_like(tot)
     for t in temps:
         t.wait()
     inv_ref[...] = LOG2E / jnp.concatenate([shp[i] for i in range(8)], axis=0)
 
     def pass_one(i, _):
-        move(9 + 6 * i, 6, 6)
-        normed = layer_norm(xv[pl.ds(i * BLK, BLK), :].astype(F32), g1[...], b1[...]).astype(BF)
-        fx_s[...] = nn(normed, w_f[...]).astype(BF)
-        xm = nn(normed, w_x[...]).astype(BF)
-        logit[...] = nt(bigp[...], xm)
-
-        def emit(hh, lb, sw):
-            tot[hh * 256 : hh * 256 + 256, :] += sw
-            swt[hh * 256 : hh * 256 + 256, lb * 128 : lb * 128 + 128] = sw.astype(BF)
-
-        slice_softmax(logit, offs, inv_ref, BLK, emit)
-        acc[...] += nn(swt[...], fx_s[...])
+        send(7 + 9 * i, 16 + 9 * i)
+        gather(16 + 14 * i, 14)
+        normed, xm = {}, {}
+
+        def norm(s):
+            x = xv[pl.ds(i * BLK + s * SUB, SUB), :].astype(F32)
+            normed[s] = layer_norm(x, g1[...], b1[...]).astype(BF)
+
+        def project(s):
+            fx_s[s * SUB : s * SUB + SUB, :] = nn(normed[s], w_f[...]).astype(BF)
+            xm[s] = nn(normed[s], w_x[...]).astype(BF)
+
+        def score(s):
+            logit[:, s * SUB : s * SUB + SUB] = nt(bigp[...], xm[s])
+
+        def weights(s):
+            def emit(hh, lb, sw):
+                tot[hh * 256 : hh * 256 + 256, :] += sw
+                swt[0, hh * 256 : hh * 256 + 256, lb * 128 : lb * 128 + 128] = sw.astype(BF)
+
+            slice_softmax(logit, offs, inv_ref, sub_lanes(s), emit)
+
+        skewed(BLK // SUB, norm, project, score, weights)
+        acc[...] += nn(swt[0], fx_s[...])
         return 0
 
     lax.fori_loop(0, ROWS // BLK, pass_one, 0)
+
+    nbr = partner(1)
+
+    def arrived(n, sem):
+        pltpu.make_async_remote_copy(
+            src_ref=xsend.at[pl.ds(0, n)], dst_ref=rows_in.at[pl.ds(0, n)], send_sem=row_send,
+            recv_sem=sem, device_id=nbr, device_id_type=MESH,
+        ).wait_recv()
+
+    def weigh(i):
+        normed, xm = {}, {}
+
+        def norm(s):
+            x = rows_in[pl.ds(i * 16, 16)].reshape(BLK, C)[s * SUB : s * SUB + SUB].astype(F32)
+            normed[s] = layer_norm(x, g1[...], b1[...]).astype(BF)
+
+        def project(s):
+            xm[s] = nn(normed[s], w_x[...]).astype(BF)
+
+        def score(s):
+            logit[:, s * SUB : s * SUB + SUB] = nt(bigp[...], xm[s])
+
+        def weights(s):
+            def emit(hh, lb, sw):
+                swt[i, hh * 256 : hh * 256 + 256, lb * 128 : lb * 128 + 128] = sw.astype(BF)
+
+            slice_softmax(logit, offs, inv_ref, sub_lanes(s), emit)
+
+        skewed(BLK // SUB, norm, project, score, weights)
+
+    def weigh_sending(first, count):
+        def step(i, _):
+            send(first + count * i, first + count + count * i)
+
+            @pl.when(i == 0)
+            def _():
+                arrived(15, row_recv.at[0])
+
+            @pl.when(i > 0)
+            def _():
+                arrived(16, row_recv.at[i])
+
+            weigh(i)
+            return 0
+
+        return step
 
     mask = head_mask()
 
@@ -250,7 +325,8 @@
     for t in first:
         t.start()
     rs[p] = pay[p]
-    move(57, 6, 10)
+    step = weigh_sending(79, 4)
+    lax.fori_loop(0, 2, step, 0)
     for t in first:
         t.wait()
     mine[...] = jnp.sum(rs[...], axis=0)
@@ -258,7 +334,7 @@
     for t in second:
         t.start()
     hd[h] = mine[...]
-    move(63, 10, 10)
+    lax.fori_loop(2, 4, step, 0)
     for t in second:
         t.wait()
     pay[0] = jnp.sum(hd[...], axis=0)
@@ -268,8 +344,8 @@
     for t in third:
         t.start()
     res[p] = pay[0]
-    move(73, 10, 45)
-    lax.fori_loop(83, DEVS, send_rows, 0)
+    send(79 + 4 * 4, DEVS)
+    lax.fori_loop(4, EARLY, weigh_sending(0, 0), 0)
     for t in third:
         t.wait()
 
@@ -296,46 +372,43 @@
     sout = tn(att, spread(v), precision=HI)
     sout_ref[...] = spread(sout).astype(BF)
 
-    nbr = partner(1)
-
-    def arrived(n, sem):
-        pltpu.make_async_remote_copy(
-            src_ref=xsend.at[pl.ds(0, n)], dst_ref=rows_in.at[pl.ds(0, n)], send_sem=row_send,
-            recv_sem=sem, device_id=nbr, device_id_type=MESH,
-        ).wait_recv()
-
-    def pass_two(i, _):
-        @pl.when(i == 0)
-        def _():
-            arrived(15, row_recv.at[0])
-
-        @pl.when(i > 0)
-        def _():
-            arrived(16, row_recv.at[i])
-
-        x = rows_in[pl.ds(i * 16, 16)].reshape(BLK, C).astype(F32)
-        normed = layer_norm(x, g1[...], b1[...]).astype(BF)
-        xm = nn(normed, w_x[...]).astype(BF)
-        logit[...] = nt(bigp[...], xm)
-
-        def emit(hh, lb, sw):
-            swt[hh * 256 : hh * 256 + 256, lb * 128 : lb * 128 + 128] = sw.astype(BF)
-
-        slice_softmax(logit, offs, inv_ref, BLK, emit)
-        o = tn(swt[...], sout_ref[...]).astype(BF)
-        y = x + nn(o, w_e[...]) + b_e[...]
-        z = layer_norm(y, g2[...], b2[...]).astype(BF)
-        u = nn(z, w_1[...]) + b_1[...]
-        g = (u * (1.0 + lax.erf(u * math.sqrt(0.5)))).astype(BF)
-        y = y + 0.5 * nn(g, w_2[...]) + b_2[...]
-        at = i * BLK * 2
-        stage[pl.ds(at, BLK, stride=2), :] = y[:, :128]
-        stage[pl.ds(at + 1, BLK, stride=2), :] = y[:, 128:]
-        rows = pl.ds(at, BLK * 2)
+    def finish(i):
+        o, y, z, g = {}, {}, {}, {}
+
+        def blend(s):
+            o[s] = tn(swt[i, :, s * FSUB : s * FSUB + FSUB], sout_ref[...]).astype(BF)
+
+        def norm(s):
+            x = rows_in[pl.ds(i * 16, 16)].reshape(BLK, C)[s * FSUB : s * FSUB + FSUB]
+            y[s] = x.astype(F32) + nn(o[s], w_e[...]) + b_e[...]
+            z[s] = layer_norm(y[s], g2[...], b2[...]).astype(BF)
+
+        def enter(s):
+            u = nn(z[s], w_1[...]) + b_1[...]
+            g[s] = (u * (1.0 + lax.erf(u * math.sqrt(0.5)))).astype(BF)
+
+        def leave(s):
+            a = y[s] + 0.5 * nn(g[s], w_2[...]) + b_2[...]
+            at = i * BLK * 2 + s * FSUB * 2
+            stage[pl.ds(at, FSUB, stride=2), :] = a[:, :128]
+            stage[pl.ds(at + 1, FSUB, stride=2), :] = a[:, 128:]
+
+        skewed(BLK // FSUB, blend, norm, enter, leave)
+        rows = pl.ds(i * BLK * 2, BLK * 2)
         pltpu.make_async_copy(stage.at[rows], y_hbm.at[rows], y_sem.at[i]).start()
-        return 0
-
-    lax.fori_loop(0, ROWS // BLK, pass_two, 0)
+
+    def finish_early(i, _):
+        finish(i)
+        return 0
+
+    def finish_late(i, _):
+        arrived(16, row_recv.at[i])
+        weigh(i)
+        finish(i)
+        return 0
+
+    lax.fori_loop(0, EARLY, finish_early, 0)
+    lax.fori_loop(EARLY, ROWS // BLK, finish_late, 0)
 
     n = DEVS - 1
     pltpu.make_async_remote_copy(
@@ -363,8 +436,9 @@
         loads[-1].start()
 
     def scatter(t, _):
+        places = lbl_ref.at[t]
         for r in range(PER):
-            flat[pl.ds(lbl_ref[t, r], 2), :] = y[pl.ds(t * PER * 2 + 2 * r, 2), :]
+            flat[pl.ds(places[r], 2), :] = y[pl.ds(t * PER * 2 + 2 * r, 2), :]
         return 0
 
     for i in range(PIECES):
@@ -402,19 +476,19 @@
             jax.ShapeDtypeStruct((ROWS * 2, 128), F32),
             jax.ShapeDtypeStruct((DEVS, 1, 128), jnp.int32),
         ],
-        in_specs=[ANY] + [VM] * (len(args) - 1),
+        in_specs=[ANY, VM, SM] + [VM] * (len(args) - 3),
         out_specs=[ANY, VM],
         scratch_shapes=[
             pltpu.VMEM((ROWS, C), BF),
             pltpu.VMEM((ROWS * 2, 128), F32),
-            pltpu.VMEM((PER * 2, 128), F32),
+            pltpu.VMEM((16 * PER * 2, 128), F32),
             pltpu.VMEM((DEVS, PER, C), BF),
             pltpu.VMEM((DEVS, PER, C), BF),
             pltpu.VMEM((DEVS, 1, 128), jnp.int32),
             pltpu.VMEM((DEVS, 128), jnp.int32),
             pltpu.SMEM((DEVS, 128), jnp.int32),
             pltpu.VMEM((SL, BLK), F32),
-            pltpu.VMEM((SL, BLK), BF),
+            pltpu.VMEM((ROWS // BLK, SL, BLK), BF),
             pltpu.VMEM((BLK, C), BF),
             pltpu.VMEM((SL, C), F32),
             pltpu.VMEM((SL, 128), F32),
@@ -426,6 +500,7 @@
             pltpu.VMEM((8, 8, 128), F32),
             pltpu.VMEM((8, 128), F32),
             pltpu.VMEM((16, 8, 128), F32),
+            pltpu.VMEM((2, 128), F32),
             pltpu.VMEM((8, 2, 128), F32),
             pltpu.VMEM((HEADS, 128), F32),
             pltpu.VMEM((SL, C), BF),
@@ -462,7 +537,7 @@
 ):
     row = lambda a: a.reshape(1, -1)
     y, lbl = exchange(
-        x, pos.reshape(48, 1, 128), jnp.broadcast_to(sharp[:, None], (2, 128)), row(g1),
+        x, pos.reshape(48, 1, 128), sharp, row(g1),
         row(b1), w_f, w_x, part, row(off), wq, wk, wv, w_e, row(b_e), row(g2), row(b2), w_1,
         row(b_1), w_2, row(b_2),
     )

time: 106 us -> 87.2 us (0.82)
  Pallas kernels: 105 us -> 86.8 us
  local copies, waits for them, and re-layouts: 1.28 us -> 0 us
    pallas_call x1, Pallas kernels: 94.7 us -> 77.1 us  [exchange(): pl.pallas_call(exchange_kernel, out_shape=[jax.ShapeDtypeStruct((ROWS * 2...]
    broadcast_in_dim x1 -> x0, local copies, waits for them, and re-layouts: 1.28 us -> none  [body(): jnp.broadcast_to(sharp[:, None], (2, 128))]
where the time goes in v3:
time: 87.2 us; the launch traced here: 87 us
  Pallas kernels  86.8 us (100%)
    pallas_call x1, Pallas kernels, exchange(): pl.pallas_call(exchange_kernel, out_shape=[jax.ShapeDtypeStruct((ROWS * 2...  77.1 us
    pallas_call x1, Pallas kernels, place_rows(): pl.pallas_call(place_kernel, out_shape=jax.ShapeDtypeStruct((ROWS, C), BF...  9.71 us

profile of v3, /device:TPU:1, one launch (start us, length us, event | category | flops | bytes accessed | tf_op | source)
XLA Modules:
  0.0 87.0 jit_solution(2655932834759226290)
XLA Ops:
  0.0 77.1 %exchange.1 = (f32[12288,128]{1,0:T(8,128)}, s32[128,1,128]{2,1,0:T(1,128)}) custom-call(bf16[6144,256]{1,0:T(8,128)(2,1)} %x_hbm.1, s32[48,1,128]{2,1,0:T(1,128)} %bitcast.12, f32[2]{0:T(128)} %sharp.1, f32[1,256]{1,0:T(1,128)} %bitcast.14, f32[1,256]{1,0:T(1,128)} %bitcast.15, bf16[256,256]{1,0:T(8,128)(2,1)} %w_f.1, bf16[256,256]{1,0:T(8,128)(2,1)} %w_x.1, ...), custom_call_target="tpu_custom_call" | custom-call | tf_op jit(solution)/shard_map/exchange/pallas_call | solution.py:473
  77.1 9.7 %place_rows.1 = bf16[6144,256]{1,0:T(8,128)(2,1)} custom-call(f32[12288,128]{1,0:T(8,128)} %get-tuple-element.7.y_hbm, s32[128,128]{1,0:T(8,128)} %bitcast.11), custom_call_target="tpu_custom_call" | custom-call | tf_op jit(solution)/shard_map/place_rows/pallas_call | solution.py:518

commit v4 on v3

--- a/solution.py
+++ b/solution.py
@@ -22,7 +22,7 @@
 BLK = 768
 SUB = 256
 FSUB = 384
-EARLY = 6
+EARLY = 4
 
 
 def iota(shape, dim):
@@ -98,7 +98,7 @@
 def exchange_kernel(
     x_hbm, pos_ref, sharp, g1, b1, w_f, w_x, part, off, wq, wk, wv, w_e, b_e, g2, b2, w_1, b_1,
     w_2, b_2, y_hbm, lbl_in,
-    xv, src, hop, xsend, rows_in, lbl, ord_v, ord_s, logit, swt, fx_s, acc, tot, bigp, offs,
+    xv, src, hop, xsend, rows_in, lbl, ord_v, ord_s, logit, swt, swr, fx_s, acc, tot, bigp, offs,
     wide, pay, rs, hd, mine, res, own_temp, shp, inv_ref, sout_ref, stage,
     x_sem, ord_sem, y_sem, row_send, row_recv, lbl_send, lbl_recv, small_send, small_recv,
 ):
@@ -106,7 +106,17 @@
     p = lax.axis_index("pts")
     z0, y0, x0, c0 = h >> 1, ((p >> 3) << 1) + (h & 1), (p >> 1) & 3, p & 1
 
+    at_z = [((z0 + i) & 3) * 2 for i in range(4)]
+    at_y = [(y0 + i) & 3 for i in range(4)]
+    at_y = [(y & 1, (y >> 1) * 8) for y in at_y]
+    at_x = [((x0 + i) & 3) * 2 for i in range(4)]
+    at_c = [(c0 + i) & 1 for i in range(2)]
+
     def partner(k):
+        if isinstance(k, int):
+            k = (k * 53) & 127
+            y = at_y[(k >> 3) & 3]
+            return at_z[k >> 5] + y[0], y[1] + at_x[(k >> 1) & 3] + at_c[k & 1]
         k = (k * 53) & 127
         z = (z0 + (k >> 5)) & 3
         y = (y0 + (k >> 3)) & 3
@@ -120,11 +130,8 @@
     own_temp[...] = jnp.concatenate(both, axis=0)
     bar = pltpu.get_barrier_semaphore()
 
-    def greet(k, _):
+    for k in range(1, DEVS):
         pl.semaphore_signal(bar, inc=1, device_id=partner(k), device_id_type=MESH)
-        return 0
-
-    lax.fori_loop(1, DEVS, greet, 0, unroll=4)
 
     before = (iota((256, 256), 0) < iota((256, 256), 1)).astype(BF)
     tri = jnp.concatenate([before, jnp.ones((256, 128), BF)], axis=1)
@@ -168,7 +175,7 @@
             device_id=dev, device_id_type=MESH,
         )
 
-    def send_rows(k, _):
+    def send_rows(k):
         dev = partner(k)
         to = dev[0] * 16 + dev[1]
         pltpu.make_async_remote_copy(
@@ -179,10 +186,10 @@
             src_ref=lbl.at[to], dst_ref=lbl_in.at[k], send_sem=lbl_send, recv_sem=lbl_recv,
             device_id=dev, device_id_type=MESH,
         ).start()
-        return 0
-
-    def send(first, stop):
-        lax.fori_loop(first, stop, send_rows, 0)
+
+    def send(first, count):
+        for k in range(count):
+            send_rows(first + k)
 
     shp[h] = own_temp[...]
     temps = [send_small(own_temp, shp.at[h], ((h + i) % 8, p), i - 1) for i in range(1, 8)]
@@ -217,7 +224,7 @@
     rows_in[0] = xsend[0]
     lbl_in[0] = lbl[h * 16 + p]
 
-    send(1, 7)
+    send(1, 6)
     bigp[...] = wide_partition(part[...])
     offs[...] = offset_rows(off[...])
     same_head = iota((C, C), 0) // DH == iota((C, C), 1) // DH
@@ -232,7 +239,7 @@
     inv_ref[...] = LOG2E / jnp.concatenate([shp[i] for i in range(8)], axis=0)
 
     def pass_one(i, _):
-        send(7 + 9 * i, 16 + 9 * i)
+        send(7 + 7 * i, 7)
         gather(16 + 14 * i, 14)
         normed, xm = {}, {}
 
@@ -250,12 +257,12 @@
         def weights(s):
             def emit(hh, lb, sw):
                 tot[hh * 256 : hh * 256 + 256, :] += sw
-                swt[0, hh * 256 : hh * 256 + 256, lb * 128 : lb * 128 + 128] = sw.astype(BF)
+                swt[hh * 256 : hh * 256 + 256, lb * 128 : lb * 128 + 128] = sw.astype(BF)
 
             slice_softmax(logit, offs, inv_ref, sub_lanes(s), emit)
 
         skewed(BLK // SUB, norm, project, score, weights)
-        acc[...] += nn(swt[0], fx_s[...])
+        acc[...] += nn(swt[...], fx_s[...])
         return 0
 
     lax.fori_loop(0, ROWS // BLK, pass_one, 0)
@@ -283,7 +290,7 @@
 
         def weights(s):
             def emit(hh, lb, sw):
-                swt[i, hh * 256 : hh * 256 + 256, lb * 128 : lb * 128 + 128] = sw.astype(BF)
+                swr[i, lb * 128 : lb * 128 + 128, hh * 256 : hh * 256 + 256] = sw.astype(BF).T
 
             slice_softmax(logit, offs, inv_ref, sub_lanes(s), emit)
 
@@ -291,7 +298,7 @@
 
     def weigh_sending(first, count):
         def step(i, _):
-            send(first + count * i, first + count + count * i)
+            send(first + count * i, count)
 
             @pl.when(i == 0)
             def _():
@@ -325,7 +332,7 @@
     for t in first:
         t.start()
     rs[p] = pay[p]
-    step = weigh_sending(79, 4)
+    step = weigh_sending(63, 2)
     lax.fori_loop(0, 2, step, 0)
     for t in first:
         t.wait()
@@ -344,10 +351,9 @@
     for t in third:
         t.start()
     res[p] = pay[0]
-    send(79 + 4 * 4, DEVS)
-    lax.fori_loop(4, EARLY, weigh_sending(0, 0), 0)
     for t in third:
         t.wait()
+    send(71, DEVS - 71)
 
     def gathered(i):
         return jnp.concatenate(
@@ -376,7 +382,7 @@
         o, y, z, g = {}, {}, {}, {}
 
         def blend(s):
-            o[s] = tn(swt[i, :, s * FSUB : s * FSUB + FSUB], sout_ref[...]).astype(BF)
+            o[s] = nn(swr[i, s * FSUB : s * FSUB + FSUB, :], sout_ref[...]).astype(BF)
 
         def norm(s):
             x = rows_in[pl.ds(i * 16, 16)].reshape(BLK, C)[s * FSUB : s * FSUB + FSUB]
@@ -488,7 +494,8 @@
             pltpu.VMEM((DEVS, 128), jnp.int32),
             pltpu.SMEM((DEVS, 128), jnp.int32),
             pltpu.VMEM((SL, BLK), F32),
-            pltpu.VMEM((ROWS // BLK, SL, BLK), BF),
+            pltpu.VMEM((SL, BLK), BF),
+            pltpu.VMEM((ROWS // BLK, BLK, SL), BF),
             pltpu.VMEM((BLK, C), BF),
             pltpu.VMEM((SL, C), F32),
             pltpu.VMEM((SL, 128), F32),

time: 87.2 us -> 82.3 us (0.944)
  Pallas kernels: 86.8 us -> 81.9 us
    pallas_call x1, Pallas kernels: 77.1 us -> 72.2 us  [exchange(): pl.pallas_call(exchange_kernel, out_shape=[jax.ShapeDtypeStruct((ROWS * 2...]
where the time goes in v4:
time: 82.3 us; the launch traced here: 82.1 us
  Pallas kernels  81.9 us (100%)
    pallas_call x1, Pallas kernels, exchange(): pl.pallas_call(exchange_kernel, out_shape=[jax.ShapeDtypeStruct((ROWS * 2...  72.2 us
    pallas_call x1, Pallas kernels, place_rows(): pl.pallas_call(place_kernel, out_shape=jax.ShapeDtypeStruct((ROWS, C), BF...  9.71 us

profile of v4, /device:TPU:1, one launch (start us, length us, event | category | flops | bytes accessed | tf_op | source)
XLA Modules:
  0.0 82.1 jit_solution(11813046441665996232)
XLA Ops:
  0.0 72.2 %exchange.1 = (f32[12288,128]{1,0:T(8,128)}, s32[128,1,128]{2,1,0:T(1,128)}) custom-call(bf16[6144,256]{1,0:T(8,128)(2,1)} %x_hbm.1, s32[48,1,128]{2,1,0:T(1,128)} %bitcast.12, f32[2]{0:T(128)} %sharp.1, f32[1,256]{1,0:T(1,128)} %bitcast.14, f32[1,256]{1,0:T(1,128)} %bitcast.15, bf16[256,256]{1,0:T(8,128)(2,1)} %w_f.1, bf16[256,256]{1,0:T(8,128)(2,1)} %w_x.1, ...), custom_call_target="tpu_custom_call" | custom-call | tf_op jit(solution)/shard_map/exchange/pallas_call | solution.py:479
  72.2 9.7 %place_rows.1 = bf16[6144,256]{1,0:T(8,128)(2,1)} custom-call(f32[12288,128]{1,0:T(8,128)} %get-tuple-element.7.y_hbm, s32[128,128]{1,0:T(8,128)} %bitcast.11), custom_call_target="tpu_custom_call" | custom-call | tf_op jit(solution)/shard_map/place_rows/pallas_call | solution.py:525
